TPU v7x, 256 devices: a whole 4x4x8 slice. The times are simulated.
256 devices in a mesh: seq: 32 (over y, z), head: 4 (over x), rep: 2 (over core).
Axes of the slice: x: 4, y: 4, z: 8, core: 2. Of those that a mesh axis runs over, the one named last changes fastest.
Arguments:
- hidden: bfloat16 [65536, 8192], P(('seq', 'rep')), may hold values from -6 to 6
- key_weight: bfloat16 [8192, 1024], P(('seq', 'rep'), 'head'), may hold values from -0.0625 to 0.0625
- value_weight: bfloat16 [8192, 1024], P(('seq', 'rep'), 'head'), may hold values from -0.0625 to 0.0625
- group_scale: float32 [2, 1024], P(None, 'head'), may hold values from 0.05 to 0.4
- new_kv: bfloat16 [4, 256, 2, 1024], P(None, 'seq', None, 'head'), may hold values from -6 to 6
- decode_query: bfloat16 [4, 256, 8192], P(None, 'seq', 'head'), may hold values from -400 to 400
- page_table: int32 [256, 32], replicated, may hold values from 0 to 2047, as said below
- lengths: int32 [256], replicated, may hold values from 1 to 1024
Outputs:
- kv_cache: bfloat16 [65536, 2, 1024], P(('seq', 'rep'), None, 'head')
- smoothing: float32 [1024], P('head')
- attention: bfloat16 [4, 256, 8192], P(None, 'seq', 'head')
Inputs may be any that keep to these rules, and one draw needn't show every extreme that they name: `page_table`: page p holds prefilled tokens p * 32 to p * 32 + 31. Slot j of request r is live when j * 32 < lengths[r]. Over the live slots of one parity of j of the 8 requests r with one value of r // 8, at most 2 pages lie in any one block of 32 consecutive pages; this bound is reached.
All inputs are finite; a program needn't handle non-finite values.
Results may differ from a plain program's by a relative error of at most 0.007.
The roundings to bfloat16 on the way count: a program that leaves them out, or rounds other values in their place, can miss the bound.
Values may be sent and summed in bfloat16 or wider, within the bound.
A program may use at most 128 MiB of HBM per device.

v0:
```python
import jax
import jax.numpy as jnp
from jax import lax
from jax.sharding import PartitionSpec as P

KVH = 8
HD = 128
QH = 64
PAGE = 32


EPSILON = 1e-05
NEGATIVE = -1e30


def side_by_side(arrays, axis, dim, along):
    ends, at = ([], 0)
    for a in arrays[:-1]:
        at += a.shape[along]
        ends.append(at)
    both = jnp.concatenate(arrays, axis=along)
    return tuple(jnp.split(lax.all_gather(both, axis, axis=dim, tiled=True), ends, axis=along))


def from_everyone(shard, axis):
    devices = lax.axis_size(axis)
    return lax.all_to_all(
        jnp.broadcast_to(shard[None], (devices, *shard.shape)), axis, 0, 0, tiled=True
    )


def of_everyone(shard, axis):
    return from_everyone(shard, axis).max(axis=0)


def collected_together(shard, axis):
    leaves = jax.tree.leaves(shard)
    order = sorted(range(len(leaves)), key=lambda k: -leaves[k].size)
    width = (1, *leaves[order[0]].shape)[-1]
    lines = [
        jnp.pad(leaves[k].reshape(-1), (0, -leaves[k].size % width)).reshape(-1, width)
        for k in order
    ]
    both, at, found = (from_everyone(jnp.concatenate(lines), axis), 0, {})
    for k, line in zip(order, lines):
        section = both[:, at : at + len(line)].reshape(len(both), -1)
        found[k] = section[:, : leaves[k].size].reshape(-1, *leaves[k].shape)
        at += len(line)
    numbers = iter(range(len(leaves)))
    return jax.tree.map(lambda _: found[next(numbers)], shard)


def combined_pairwise(pieces, combine):
    while len(jax.tree.leaves(pieces)[0]) > 1:
        pieces = jax.vmap(combine)(
            *(jax.tree.map(lambda part: part[side::2], pieces) for side in (0, 1))
        )
    return jax.tree.map(lambda part: part[0], pieces)


def joined_all(shard, axis, combine):
    pieces = collected_together(shard, axis)
    return combined_pairwise(pieces, combine)


def clipped(raw_keys, raw_values, smooth, group_scale):
    keys_out = jnp.clip(raw_keys / smooth, -8.0 * group_scale[0], 7.0 * group_scale[0])
    values_out = jnp.clip(raw_values, -8.0 * group_scale[1], 7.0 * group_scale[1])
    return (keys_out, values_out)


def combine(earlier, latter):
    highest = jnp.maximum(earlier[0], latter[0])
    left_scale = jnp.exp(earlier[0] - highest)
    right_scale = jnp.exp(latter[0] - highest)
    return (
        highest,
        earlier[1] * left_scale + latter[1] * right_scale,
        earlier[2] * left_scale[..., None] + latter[2] * right_scale[..., None],
    )


def on_device(
    hidden, key_weight, value_weight, group_scale, new_kv, decode_query, page_table, lengths
):
    tokens = hidden.shape[0]
    columns = key_weight.shape[1]
    heads_kv = columns // HD
    group_size = QH // KVH
    pieces = side_by_side((key_weight, value_weight), ("seq", "rep"), 0, 1)
    raw_keys = jnp.dot(hidden, pieces[0], preferred_element_type=jnp.float32)
    raw_values = jnp.dot(hidden, pieces[1], preferred_element_type=jnp.float32)
    local_max = jnp.max(jnp.abs(raw_keys), axis=0)
    smoothing = jnp.sqrt(of_everyone(local_max, ("seq", "rep")) + EPSILON)
    keys_clip, values_clip = clipped(raw_keys, raw_values, smoothing, group_scale)
    kv_cache = jnp.stack([keys_clip, values_clip], axis=1).astype(jnp.bfloat16)
    groups = lax.axis_size("seq")
    owners = lax.axis_size("rep")
    sources = groups * owners
    pages_dev = tokens // PAGE
    requests = page_table.shape[0]
    slot_count = page_table.shape[1]
    per_group = requests // groups
    entries = per_group * slot_count
    capacity = entries // (owners * sources)
    page_pool = kv_cache.reshape(pages_dev, PAGE, 2, columns)
    slot_ids = jnp.arange(slot_count, dtype=jnp.int32)
    live_slots = (slot_ids[None, :] * PAGE < lengths[:, None]).reshape(groups, entries)
    owner_of = jnp.broadcast_to(slot_ids % owners, (requests, slot_count)).reshape(groups, entries)
    source_of = (page_table // pages_dev).reshape(groups, entries)
    local_of = (page_table % pages_dev).reshape(groups, entries)
    my_index = lax.axis_index(("seq", "rep"))
    owner_hot = owner_of[:, None, :] == jnp.arange(owners, dtype=jnp.int32)[None, :, None]
    sending = live_slots[:, None, :] & owner_hot & (source_of == my_index)[:, None, :]
    send_rank = jnp.cumsum(sending.astype(jnp.int32), axis=2) - 1
    chosen = sending[:, :, None, :] & (
        send_rank[:, :, None, :] == jnp.arange(capacity, dtype=jnp.int32)[None, None, :, None]
    )
    send_page = jnp.sum(jnp.where(chosen, local_of[:, None, None, :], 0), axis=3)
    send_live = jnp.any(chosen, axis=3)
    outgoing = jnp.where(
        send_live[..., None, None, None], page_pool[send_page], jnp.zeros((), jnp.bfloat16)
    )
    incoming = lax.all_to_all(
        outgoing.reshape((sources,) + outgoing.shape[2:]),
        ("seq", "rep"),
        split_axis=0,
        concat_axis=0,
        tiled=True,
    )
    received = incoming.reshape((sources * capacity,) + incoming.shape[-3:])
    my_group = lax.axis_index("seq")
    my_owner = lax.axis_index("rep")
    mine_table = lax.dynamic_slice_in_dim(page_table, my_group * per_group, per_group, 0)
    mine_length = lax.dynamic_slice_in_dim(lengths, my_group * per_group, per_group, 0)
    half_slots = slot_count // owners
    owned_table = lax.dynamic_index_in_dim(
        mine_table.reshape(per_group, half_slots, owners), my_owner, 2, keepdims=False
    )
    owned_slot = jnp.arange(half_slots, dtype=jnp.int32) * owners + my_owner
    owned_live = owned_slot[None, :] * PAGE < mine_length[:, None]
    owned_source = (owned_table // pages_dev).reshape(-1)
    flat_live = owned_live.reshape(-1)
    source_hot = (
        owned_source[:, None] == jnp.arange(sources, dtype=jnp.int32)[None, :]
    ) & flat_live[:, None]
    running = jnp.cumsum(source_hot.astype(jnp.int32), axis=0)
    arrival = jnp.sum(jnp.where(source_hot, running, 0), axis=1) - 1
    slot_index = jnp.where(flat_live, owned_source * capacity + arrival, 0)
    owned_pages = received[slot_index].reshape(per_group, half_slots * PAGE, 2, columns)
    position = (owned_slot[:, None] * PAGE + jnp.arange(PAGE, dtype=jnp.int32)[None, :]).reshape(-1)
    valid_keys = position[None, :] < mine_length[:, None]
    score_scale = HD ** (-0.5)
    smooth_query = jnp.repeat(smoothing.reshape(heads_kv, HD), group_size, axis=0).reshape(-1)
    queries = (decode_query.astype(jnp.float32) * smooth_query).astype(jnp.bfloat16)
    step_count = queries.shape[0]
    queries = queries.reshape(step_count, per_group, heads_kv, group_size, HD)
    cache_keys = owned_pages[:, :, 0].reshape(per_group, -1, heads_kv, HD)
    cache_values = owned_pages[:, :, 1].reshape(per_group, -1, heads_kv, HD)
    scores = (
        jnp.einsum("trkgd,rnkd->rktgn", queries, cache_keys, preferred_element_type=jnp.float32)
        * score_scale
    )
    key_mask = valid_keys[:, None, None, None, :]
    scores = jnp.where(key_mask, scores, NEGATIVE)
    row_max = jnp.max(scores, axis=-1)
    weights = jnp.where(key_mask, jnp.exp(scores - row_max[..., None]), 0.0)
    row_total = jnp.sum(weights, axis=-1)
    summed = jnp.einsum(
        "rktgn,rnkd->rktgd",
        weights.astype(jnp.bfloat16),
        cache_values,
        preferred_element_type=jnp.float32,
    )
    merged = joined_all((row_max, row_total, summed), "rep", combine)
    fresh_keys, fresh_values = clipped(
        new_kv[:, :, 0].astype(jnp.float32),
        new_kv[:, :, 1].astype(jnp.float32),
        smoothing,
        group_scale,
    )
    fresh_keys = fresh_keys.astype(jnp.bfloat16).reshape(step_count, per_group, heads_kv, HD)
    fresh_values = fresh_values.astype(jnp.bfloat16).reshape(step_count, per_group, heads_kv, HD)
    fresh_scores = (
        jnp.einsum("trkgd,urkd->rktgu", queries, fresh_keys, preferred_element_type=jnp.float32)
        * score_scale
    )
    causal = jnp.arange(step_count)[None, :] <= jnp.arange(step_count)[:, None]
    causal_mask = causal[None, None, :, None, :]
    fresh_scores = jnp.where(causal_mask, fresh_scores, NEGATIVE)
    fresh_max = jnp.max(fresh_scores, axis=-1)
    fresh_weights = jnp.where(causal_mask, jnp.exp(fresh_scores - fresh_max[..., None]), 0.0)
    fresh_total = jnp.sum(fresh_weights, axis=-1)
    fresh_summed = jnp.einsum(
        "rktgu,urkd->rktgd",
        fresh_weights.astype(jnp.bfloat16),
        fresh_values,
        preferred_element_type=jnp.float32,
    )
    final_max, final_total, final_summed = combine(merged, (fresh_max, fresh_total, fresh_summed))
    attention = (final_summed / final_total[..., None]).astype(jnp.bfloat16)
    attention = attention.transpose(2, 0, 1, 3, 4).reshape(
        step_count, per_group, heads_kv * group_size * HD
    )
    return (kv_cache, smoothing, attention)


def solution(mesh):
    placed = (
        P(("seq", "rep"), None),
        P(("seq", "rep"), "head"),
        P(("seq", "rep"), "head"),
        P(None, "head"),
        P(None, "seq", None, "head"),
        P(None, "seq", "head"),
        P(),
        P(),
    )
    return jax.shard_map(
        on_device,
        mesh=mesh,
        in_specs=placed,
        out_specs=(P(("seq", "rep"), None, "head"), P("head"), P(None, "seq", "head")),
        check_vma=False,
    )
```

profile of v0, /device:TPU:1, one launch (start us, length us, event | category | flops | bytes accessed | tf_op | source)
XLA Modules:
  0.0 272.9 jit_solution(5453433547613213167)
XLA Ops:
  7.2 1.5 pad_maximum_fusion.3
  8.8 0.8 fusion.45
  9.6 0.1 copy.77
  9.7 0.1 eq.80
  9.8 0.1 eq.76
  9.9 0.8 lt.136
  10.7 0.1 lt.137
  10.8 0.1 lt.144
  10.9 0.1 lt.138
  11.0 0.8 add_select_fusion
  11.8 0.1 copy.90
  11.9 0.1 broadcast_in_dim.146
  12.0 0.1 broadcast_in_dim.143
  12.3 1.2 reduce-window.6
  13.5 0.1 copy.81
  14.0 0.2 select_reduce_fusion
  14.1 0.1 copy.91
  14.3 0.2 reshape.569
  14.4 0.2 fusion.27
  14.6 0.1 copy.84
  14.7 0.1 broadcast_in_dim.144
  14.8 0.1 copy.85
  14.9 0.8 slice_multiply_fusion.3
  15.7 82.9 %all-gather.2.cloned.1.call-done = bf16[8192,512]{1,0:T(8,128)(2,1)} async-done(((bf16[128,512]{1,0:T(8,128)(2,1)}), bf16[8192,512]{1,0:T(8,128)(2,1)}) %all-gather.2.cloned.1.call-update) | async-done | bytes 8388624 | tf_op jit(solution)/shard_map/all_gather | solution.py:22
  98.6 9.5 %abs_reduce_fusion = (f32[256]{0:T(256)S(1)}, f32[256,1024]{1,0:T(8,128)S(1)}) fusion(bf16[1024,8192]{1,0:T(8,128)(2,1)} %param.8, bf16[8192,512]{1,0:T(8,128)(2,1)} %all-gather.2.cloned.1.call-done), kind=kOutput, calls=%fused_computation.23 | convolution fusion | flops 4295491584 | bytes 22021120 | tf_op jit(solution)/shard_map/dot_general | solution.py:91
  108.2 0.7 broadcast_in_dim.137
  108.8 5.7 %all-to-all-start = ((f32[64,1,256]{2,1,0:T(1,128)}), f32[64,1,256]{2,1,0:T(1,128)S(1)}, u32[]{:S(2)}, u32[]{:S(2)}) async-start(f32[64,1,256]{2,1,0:T(1,128)} %broadcast_in_dim.137), calls=%async_computation | async-start | bytes 131072 | tf_op jit(solution)/shard_map/all_to_all | solution.py:27
  114.6 11.6 %fusion.11 = bf16[256,1024]{1,0:T(8,128)(2,1)S(1)} fusion(bf16[1024,8192]{1,0:T(8,128)(2,1)} %param.8, bf16[8192,512]{1,0:T(8,128)(2,1)} %all-gather.2.cloned.1.call-done, f32[256]{0:T(256)S(1)} %bitcast.135, f32[256]{0:T(256)S(1)} %bitcast.137), kind=kOutput, calls=%fused_computation.11 | convolution fusion | flops 4296278016 | bytes 21497856 | tf_op jit(solution)/shard_map/dot_general | solution.py:92
  126.2 0.2 copy.87
  126.4 0.1 reduce_max.37
  126.5 0.2 fusion.77
  126.7 1.0 copy.86
  127.7 1.1 pad_maximum_fusion.1
  128.9 2.7 %gather_fusion = bf16[128,32,2,256]{3,1,2,0:T(8,128)(2,1)} fusion(bf16[32,32,2,256]{3,1,2,0:T(8,128)(2,1)S(1)} %pad_maximum_fusion.1, s32[1024]{0:T(1024)S(1)} %pad_clamp_fusion.1), kind=kCustom, calls=%fused_computation | custom fusion | bytes 8389120 | tf_op jit(solution)/shard_map/gather | solution.py:122
  131.6 4.5 %broadcast_select_fusion = bf16[64,2,32,2,256]{4,2,3,1,0:T(8,128)(2,1)} fusion(bf16[64,2,32,2,256]{4,2,3,1,0:T(8,128)(2,1)} %bitcast.101, pred[64,2]{1,0:T(8,128)(4,1)S(1)} %copy.85), kind=kLoop, calls=%fused_computation.6 | loop fusion | flops 2097152 | bytes 8388736 | tf_op jit(solution)/shard_map/jit(_where)/select_n | solution.py:121
  136.1 10.6 %all-to-all-start.1 = ((bf16[64,2,32,2,256]{4,2,3,1,0:T(8,128)(2,1)}), bf16[64,2,32,2,256]{4,2,3,1,0:T(8,128)(2,1)}, u32[]{:S(2)}, u32[]{:S(2)}) async-start(bf16[64,2,32,2,256]{4,2,3,1,0:T(8,128)(2,1)} %broadcast_select_fusion), calls=%async_computation.1 | async-start | bytes 8388608 | tf_op jit(solution)/shard_map/all_to_all | solution.py:124
  147.0 0.1 lt.152
  147.1 0.1 lt.154
  147.5 0.1 fusion.41
  147.6 0.2 reduce_window_sum.29
  148.0 0.2 select_reduce_fusion.1
  148.3 0.2 fusion.78
  148.5 0.1 pad_maximum_fusion
  148.6 2.0 copy.104
  150.7 0.7 fusion.71
  151.4 0.2 fusion.30
  151.6 91.0 %all-to-all-done.1 = bf16[64,2,32,2,256]{4,2,3,1,0:T(8,128)(2,1)} async-done(((bf16[64,2,32,2,256]{4,2,3,1,0:T(8,128)(2,1)}), bf16[64,2,32,2,256]{4,2,3,1,0:T(8,128)(2,1)}, u32[]{:S(2)}, u32[]{:S(2)}) %all-to-all-start.1) | async-done | bytes 4194336 | tf_op jit(solution)/shard_map/all_to_all | solution.py:124
  242.6 5.0 %gather_fusion.1 = bf16[128,32,2,256]{3,1,2,0:T(8,128)(2,1)} fusion(bf16[128,32,2,256]{3,1,2,0:T(8,128)(2,1)} %bitcast.18, s32[1024]{0:T(1024)S(1)} %pad_clamp_fusion), kind=kCustom, calls=%fused_computation.1 | custom fusion | bytes 8389120 | tf_op jit(solution)/shard_map/gather | solution.py:150
  247.6 2.6 copy.94
  250.3 2.2 fusion.67
  252.5 2.9 %copy.95 = bf16[8,512,1,256]{1,3,0,2:T(8,128)(2,1)S(1)} copy(bf16[8,512,1,256]{3,1,0,2:T(8,128)(2,1)} %get-tuple-element.21) | data formatting | bytes 4194304 | tf_op jit(solution)/shard_map/slice | solution.py:158
  255.3 0.5 fusion.70
  255.9 0.1 reshape.562
  256.0 0.4 fusion.19
  256.3 0.1 reshape.563
  256.4 2.9 %copy.98 = bf16[8,512,1,256]{1,3,0,2:T(8,128)(2,1)S(1)} copy(bf16[8,512,1,256]{3,1,0,2:T(8,128)(2,1)} %get-tuple-element.20) | data formatting | bytes 4194304 | tf_op jit(solution)/shard_map/slice | solution.py:159
  259.3 0.8 fusion.21
  260.2 4.0 %all_to_all.16 = f32[2,520,128]{2,1,0:T(8,128)S(1)} all-to-all(f32[2,520,128]{2,1,0:T(8,128)S(1)} %broadcast_in_dim.153), channel_id=1, replica_groups=mesh['seq'=32,'head'=4,'rep'=2] {'rep'}, dimensions={0} | all-to-all | bytes 1064960 | tf_op jit(solution)/shard_map/all_to_all | solution.py:27
  264.2 0.1 slice.100
  264.3 0.1 slice.98
  264.4 0.1 slice.90
  264.5 0.1 slice.92
  264.7 0.6 fusion.17
  265.3 0.7 reshape.564
  (65 shorter events, 1.7 us)
Async XLA Ops:
  7.2 91.5 %all-gather.2.cloned.1.call-start = ((), (), s32[]{:S(2)}) async-start(), calls=%async_computation.3 | async-start | bytes 8519680 | tf_op jit(solution)/shard_map/all_gather | solution.py:22
  108.8 17.6 %all-to-all-start = ((f32[64,1,256]{2,1,0:T(1,128)}), f32[64,1,256]{2,1,0:T(1,128)S(1)}, u32[]{:S(2)}, u32[]{:S(2)}) async-start(f32[64,1,256]{2,1,0:T(1,128)} %broadcast_in_dim.137), calls=%async_computation | async-start | bytes 131072 | tf_op jit(solution)/shard_map/all_to_all | solution.py:27
  126.5 21.8 %copy-start.3 = (f32[256]{0:T(256)}, f32[256]{0:T(256)S(1)}, u32[]{:S(2)}) copy-start(f32[256]{0:T(256)S(1)} %add_sqrt_fusion) | copy-start | bytes 3076
  136.1 10.7 %copy-start.4 = (s32[256]{0:T(256)S(1)}, s32[256]{0:T(256)}, u32[]{:S(2)}) copy-start(s32[256]{0:T(256)} %param.15) | copy-start | bytes 3076
  136.1 11.0 %copy-start = (s32[256,32]{0,1:T(8,128)S(1)}, s32[256,32]{0,1:T(8,128)}, u32[]{:S(2)}) copy-start(s32[256,32]{0,1:T(8,128)} %param.14) | copy-start | bytes 98308
  136.1 12.1 %copy-start.2 = (bf16[4,8,2,256]{3,2,1,0:T(2,128)(2,1)S(1)}, bf16[4,8,2,256]{3,2,1,0:T(2,128)(2,1)}, u32[]{:S(2)}) copy-start(bf16[4,8,2,256]{3,2,1,0:T(2,128)(2,1)} %param.12) | copy-start | bytes 98308
  136.1 106.5 %all-to-all-start.1 = ((bf16[64,2,32,2,256]{4,2,3,1,0:T(8,128)(2,1)}), bf16[64,2,32,2,256]{4,2,3,1,0:T(8,128)(2,1)}, u32[]{:S(2)}, u32[]{:S(2)}) async-start(bf16[64,2,32,2,256]{4,2,3,1,0:T(8,128)(2,1)} %broadcast_select_fusion), calls=%async_computation.1 | async-start | bytes 8388608 | tf_op jit(solution)/shard_map/all_to_all | solution.py:124
  146.8 3.9 %copy-start.1 = (bf16[4,8,2048]{2,1,0:T(8,128)(2,1)S(1)}, bf16[4,8,2048]{2,1,0:T(8,128)(2,1)}, u32[]{:S(2)}) copy-start(bf16[4,8,2048]{2,1,0:T(8,128)(2,1)} %param.13) | copy-start | bytes 393220
  147.9 99.7 %copy-start.5 = (pred[4,4]{1,0:T(4,128)(4,1)}, pred[4,4]{1,0:T(4,128)(4,1)S(1)}, u32[]{:S(2)}) copy-start(pred[4,4]{1,0:T(4,128)(4,1)S(1)} %iota_compare_fusion.4) | copy-start | bytes 52
  259.3 5.4 %copy-start.6 = (pred[4,4]{1,0:T(4,128)(4,1)S(1)}, pred[4,4]{1,0:T(4,128)(4,1)}, u32[]{:S(2)}) copy-start(pred[4,4]{1,0:T(4,128)(4,1)} %copy-done.5) | copy-start | bytes 52
Sparse Core Ops, SparseCore 0:
  11.3 87.2 all-gather.1
where the time goes:
time: 274 us; the launch traced here: 273 us
  waiting for transfers between devices  174 us (64%)
  local copies, waits for them, and re-layouts  27.1 us (10%)
  matrix products  23.7 us (9%)
  starting transfers between devices  16.4 us (6%)
  between operations  14.5 us (5%)
  other arithmetic  13.2 us (5%)
  blocking collectives  4 us (1%)
    all_to_all x1, waiting for transfers between devices, on_device(): lax.all_to_all(outgoing.reshape((sources,) + outgoing.shape[2:]), ('seq',...  91 us
    all_gather x1, waiting for transfers between devices, side_by_side(): lax.all_gather(both, axis, axis=dim, tiled=True)  82.9 us
    dot_general x1, matrix products, on_device(): raw_values = jnp.dot(hidden, pieces[1], preferred_element_type=jnp.float32)  11.6 us
    all_to_all x1, starting transfers between devices, on_device(): lax.all_to_all(outgoing.reshape((sources,) + outgoing.shape[2:]), ('seq',...  10.6 us
    dot_general x1, matrix products, on_device(): raw_keys = jnp.dot(hidden, pieces[0], preferred_element_type=jnp.float32)  9.52 us
    gather x2, local copies, waits for them, and re-layouts, on_device(): received[slot_index].reshape(per_group, half_slots * PAGE, 2, columns)  7.6 us
    all_to_all x1, starting transfers between devices, from_everyone(): lax.all_to_all(jnp.broadcast_to(shard[None], (devices, *shard.shape)), ax...  5.73 us
  transfers between devices with their start and end apart: 3, of which 2 were waited for; matrix products, arithmetic and copies ran while one was open for 9% of the time, Pallas kernels for 0%

commit v1 on v0

--- a/solution.py
+++ b/solution.py
@@ -1,25 +1,316 @@
+import functools
+
 import jax
 import jax.numpy as jnp
 from jax import lax
+from jax.experimental import pallas as pl
+from jax.experimental.pallas import tpu as pltpu
 from jax.sharding import PartitionSpec as P
 
 KVH = 8
 HD = 128
 QH = 64
 PAGE = 32
+NY = 4
+NZ = 8
+CHIPS = NY * NZ
 
 
 EPSILON = 1e-05
 NEGATIVE = -1e30
 
 
-def side_by_side(arrays, axis, dim, along):
-    ends, at = ([], 0)
-    for a in arrays[:-1]:
-        at += a.shape[along]
-        ends.append(at)
-    both = jnp.concatenate(arrays, axis=along)
-    return tuple(jnp.split(lax.all_gather(both, axis, axis=dim, tiled=True), ends, axis=along))
+class Torus:
+    def __init__(self):
+        seq = lax.axis_index("seq")
+        self.y, self.z = lax.div(seq, NZ), lax.rem(seq, NZ)
+        self.core = lax.axis_index("rep")
+
+    def at(self, dy, dz):
+        y = lax.rem(self.y + (dy + NY), NY)
+        z = lax.rem(self.z + (dz + NZ), NZ)
+        return y * NZ + z
+
+
+class Stream:
+    def __init__(self, torus, number, block, send_sem, recv_sem, swap):
+        self.torus, self.number, self.block = torus, number, block
+        self.send_sem, self.recv_sem, self.swap = send_sem, recv_sem, swap
+
+    def copy(self, blk, dy, dz):
+        ref = self.block(blk, self.torus.core)
+        return pltpu.make_async_remote_copy(
+            src_ref=ref,
+            dst_ref=ref,
+            send_sem=self.send_sem,
+            recv_sem=self.recv_sem.at[blk],
+            device_id={"seq": self.torus.at(dy, dz)},
+            device_id_type=pl.DeviceIdType.MESH,
+        )
+
+    def across(self, blk):
+        if self.swap is None:
+            return
+        ref = self.block(blk, self.torus.core)
+        pltpu.make_async_remote_copy(
+            src_ref=ref,
+            dst_ref=ref,
+            send_sem=self.swap[0],
+            recv_sem=self.swap[1],
+            device_id={"rep": 1 - self.torus.core},
+            device_id_type=pl.DeviceIdType.MESH,
+        ).start()
+
+    def arrived(self, dy, dz):
+        blk = self.torus.at(dy, dz)
+        self.copy(blk, 1, 0).wait_recv()
+        return blk
+
+    def along_z(self, blk, right, left):
+        if right:
+            self.copy(blk, 0, 1).start()
+        if left:
+            self.copy(blk, 0, -1).start()
+
+    def along_y(self, blk, up, down):
+        if up:
+            self.copy(blk, 1, 0).start()
+        if down:
+            self.copy(blk, -1, 0).start()
+
+    def step_z_first(self, st):
+        turn_right = self.number % 2 == 0
+        far = -4 if turn_right else 4
+        reach = [[0], [-1, 1], [-2, 2], [-3, 3], [far]]
+        if st == 0:
+            blk = self.torus.at(0, 0)
+            self.along_z(blk, True, True)
+            self.along_y(blk, True, True)
+            self.across(blk)
+        if 1 <= st <= 4:
+            for dz in reach[st]:
+                blk = self.arrived(0, dz)
+                onward = st < 3 or (st == 3 and (dz < 0) == turn_right)
+                self.along_z(blk, onward and dz < 0, onward and dz > 0)
+                self.along_y(blk, True, True)
+                self.across(blk)
+        if 1 <= st <= 5:
+            for dz in reach[st - 1]:
+                for dy in (-1, 1):
+                    blk = self.arrived(dy, dz)
+                    even = dz % 2 == 0
+                    self.along_y(blk, even and dy < 0, not even and dy > 0)
+                    self.across(blk)
+        if 2 <= st <= 6:
+            for dz in reach[st - 2]:
+                self.across(self.arrived(2, dz))
+
+    def step_y_first(self, st):
+        even = self.number % 2 == 0
+        if st == 0:
+            blk = self.torus.at(0, 0)
+            self.along_z(blk, True, True)
+            self.along_y(blk, True, True)
+            self.across(blk)
+        if st == 1:
+            for dy in (-1, 1):
+                blk = self.arrived(dy, 0)
+                self.along_y(blk, even and dy < 0, not even and dy > 0)
+                self.along_z(blk, True, True)
+                self.across(blk)
+        if st == 2:
+            blk = self.arrived(2, 0)
+            self.along_z(blk, True, True)
+            self.across(blk)
+        for dy, first in ((0, 0), (-1, 1), (1, 1), (2, 2)):
+            k = st - first
+            turn_right = (self.number + dy) % 2 == 0
+            if 1 <= k <= 3:
+                for dz in (-k, k):
+                    blk = self.arrived(dy, dz)
+                    onward = k < 3 or (dz < 0) == turn_right
+                    self.along_z(blk, onward and dz < 0, onward and dz > 0)
+                    self.across(blk)
+            if k == 4:
+                self.across(self.arrived(dy, -4 if turn_right else 4))
+
+    def step(self, st):
+        @pl.when(self.torus.core == 0)
+        def _():
+            self.step_z_first(st)
+
+        @pl.when(self.torus.core == 1)
+        def _():
+            self.step_y_first(st)
+
+    def swap_copy(self, refs):
+        return pltpu.make_async_remote_copy(
+            src_ref=refs,
+            dst_ref=refs,
+            send_sem=self.swap[0],
+            recv_sem=self.swap[1],
+            device_id={"rep": 1 - self.torus.core},
+            device_id_type=pl.DeviceIdType.MESH,
+        )
+
+    def sent_copy(self, refs):
+        return pltpu.make_async_remote_copy(
+            src_ref=refs,
+            dst_ref=refs,
+            send_sem=self.send_sem,
+            recv_sem=self.recv_sem.at[0],
+            device_id={"rep": 1 - self.torus.core},
+            device_id_type=pl.DeviceIdType.MESH,
+        )
+
+
+STEPS_GATHER = 7
+
+
+def greet(torus):
+    barrier = pltpu.get_barrier_semaphore()
+    for dy, dz in ((1, 0), (-1, 0), (0, 1), (0, -1)):
+        pl.semaphore_signal(
+            barrier,
+            inc=1,
+            device_id={"seq": torus.at(dy, dz)},
+            device_id_type=pl.DeviceIdType.MESH,
+        )
+    pl.semaphore_signal(
+        barrier,
+        inc=1,
+        device_id={"rep": 1 - torus.core},
+        device_id_type=pl.DeviceIdType.MESH,
+    )
+    pl.semaphore_wait(barrier, 5)
+
+
+def project_kernel(
+    hidden_hbm, wk_hbm, wv_hbm, scale_ref,
+    keys_ref, values_ref, smooth_ref,
+    hid, wk, wv, mx, acc,
+    local_sem, hid_sem, send_sem, recv_sem, swap_sem,
+):
+    torus = Torus()
+    me, core = torus.at(0, 0), torus.core
+    tokens = hidden_hbm.shape[0]
+    depth = hidden_hbm.shape[1]
+    parts = 4
+    width = depth // parts
+    own_k = pltpu.make_async_copy(wk_hbm, wk.at[me, core], local_sem.at[0])
+    own_v = pltpu.make_async_copy(wv_hbm, wv.at[me, core], local_sem.at[1])
+    own_k.start()
+    own_v.start()
+    hid_copies = [
+        pltpu.make_async_copy(
+            hidden_hbm.at[:, pl.ds(k * width, width)],
+            hid.at[:, pl.ds(k * width, width)],
+            hid_sem.at[k],
+        )
+        for k in range(parts)
+    ]
+    for copy in hid_copies:
+        copy.start()
+    greet(torus)
+    own_k.wait()
+
+    def stream(number, refs, swap=True):
+        return Stream(
+            torus,
+            number,
+            lambda blk, c: refs.at[blk, c],
+            send_sem.at[number],
+            recv_sem.at[number],
+            (swap_sem.at[number, 0], swap_sem.at[number, 1]) if swap else None,
+        )
+
+    s_k, s_v, s_m = stream(0, wk), stream(1, wv), stream(2, mx)
+    rows = 512
+
+    def multiply(weights, out, k):
+        if k == 0:
+            out[...] = jnp.zeros_like(out)
+        blocks = weights.shape[0] // parts
+
+        def one(m, carry):
+            at = pl.ds(pl.multiple_of(m * rows, rows), rows)
+            w = weights[k * blocks : (k + 1) * blocks].reshape(width, weights.shape[3])
+            out[at, :] += jnp.dot(
+                hid[at, k * width : (k + 1) * width], w, preferred_element_type=jnp.float32
+            )
+            return carry
+
+        lax.fori_loop(0, tokens // rows, one, 0)
+
+    lag = {0: 0, 1: 3, 2: 9}
+    for i in range(9 + STEPS_GATHER):
+        if i == lag[1]:
+            own_v.wait()
+        for s in (s_k, s_v, s_m):
+            st = i - lag[s.number]
+            if 0 <= st < STEPS_GATHER:
+                s.step(st)
+        if i == 6:
+            s_k.swap_copy(wk.at[:, 1 - core]).wait_recv()
+        if i in (7, 8):
+            for k in ((0, 1) if i == 7 else (2, 3)):
+                hid_copies[k].wait()
+                multiply(wk, acc.at[0], k)
+        if i == 8:
+            mx[me, core] = jnp.max(
+                jnp.abs(acc[0]).reshape(tokens // 8, 8, acc.shape[2]), axis=0
+            )
+        if i == 9:
+            s_v.swap_copy(wv.at[:, 1 - core]).wait_recv()
+        if i in (10, 11, 12, 13):
+            multiply(wv, acc.at[1], i - 10)
+        if i == 14:
+            values_ref[...] = jnp.clip(
+                acc[1], -8.0 * scale_ref[1:2, :], 7.0 * scale_ref[1:2, :]
+            ).astype(jnp.bfloat16)
+    s_m.swap_copy(mx.at[:, 1 - core]).wait_recv()
+    peak = jnp.max(mx[...].reshape(2 * CHIPS, 8, mx.shape[3]), axis=0)
+    smooth = jnp.sqrt(jnp.max(peak, axis=0, keepdims=True) + EPSILON)
+    smooth_ref[...] = smooth
+    keys_ref[...] = jnp.clip(
+        acc[0] / smooth, -8.0 * scale_ref[0:1, :], 7.0 * scale_ref[0:1, :]
+    ).astype(jnp.bfloat16)
+    for s, refs in ((s_k, wk), (s_v, wv), (s_m, mx)):
+        s.sent_copy(refs.at[pl.ds(0, CHIPS - 1), core]).wait_send()
+        s.swap_copy(refs.at[:, core]).wait_send()
+
+
+def project(hidden, key_weight, value_weight, group_scale):
+    tokens, depth = hidden.shape
+    rows, columns = key_weight.shape
+    any_spec = pl.BlockSpec(memory_space=pl.ANY)
+    vmem = pl.BlockSpec(memory_space=pltpu.VMEM)
+    return pl.pallas_call(
+        project_kernel,
+        out_shape=(
+            jax.ShapeDtypeStruct((tokens, columns), jnp.bfloat16),
+            jax.ShapeDtypeStruct((tokens, columns), jnp.bfloat16),
+            jax.ShapeDtypeStruct((1, columns), jnp.float32),
+        ),
+        in_specs=[any_spec, any_spec, any_spec, vmem],
+        out_specs=(vmem, vmem, vmem),
+        scratch_shapes=[
+            pltpu.VMEM((tokens, depth), jnp.bfloat16),
+            pltpu.VMEM((CHIPS, 2, rows, columns), jnp.bfloat16),
+            pltpu.VMEM((CHIPS, 2, rows, columns), jnp.bfloat16),
+            pltpu.VMEM((CHIPS, 2, 8, columns), jnp.float32),
+            pltpu.VMEM((2, tokens, columns), jnp.float32),
+            pltpu.SemaphoreType.DMA((2,)),
+            pltpu.SemaphoreType.DMA((4,)),
+            pltpu.SemaphoreType.DMA((3,)),
+            pltpu.SemaphoreType.DMA((3, CHIPS)),
+            pltpu.SemaphoreType.DMA((3, 2)),
+        ],
+        compiler_params=pltpu.CompilerParams(
+            collective_id=0, has_side_effects=True, vmem_limit_bytes=50 * 2**20
+        ),
+        name="project",
+    )(hidden, key_weight, value_weight, group_scale)
 
 
 def from_everyone(shard, axis):
@@ -27,10 +318,6 @@
     return lax.all_to_all(
         jnp.broadcast_to(shard[None], (devices, *shard.shape)), axis, 0, 0, tiled=True
     )
-
-
-def of_everyone(shard, axis):
-    return from_everyone(shard, axis).max(axis=0)
 
 
 def collected_together(shard, axis):
@@ -87,13 +374,9 @@
     columns = key_weight.shape[1]
     heads_kv = columns // HD
     group_size = QH // KVH
-    pieces = side_by_side((key_weight, value_weight), ("seq", "rep"), 0, 1)
-    raw_keys = jnp.dot(hidden, pieces[0], preferred_element_type=jnp.float32)
-    raw_values = jnp.dot(hidden, pieces[1], preferred_element_type=jnp.float32)
-    local_max = jnp.max(jnp.abs(raw_keys), axis=0)
-    smoothing = jnp.sqrt(of_everyone(local_max, ("seq", "rep")) + EPSILON)
-    keys_clip, values_clip = clipped(raw_keys, raw_values, smoothing, group_scale)
-    kv_cache = jnp.stack([keys_clip, values_clip], axis=1).astype(jnp.bfloat16)
+    keys_clip, values_clip, smoothing = project(hidden, key_weight, value_weight, group_scale)
+    smoothing = smoothing.reshape(columns)
+    kv_cache = jnp.stack([keys_clip, values_clip], axis=1)
     groups = lax.axis_size("seq")
     owners = lax.axis_size("rep")
     sources = groups * owners

time: 274 us -> 209 us (0.76)
  waiting for transfers between devices: 174 us -> 91.2 us
  Pallas kernels: 0 us -> 65.9 us
  matrix products: 23.7 us -> 2.6 us
  between operations: 14.5 us -> 1.07 us
  starting transfers between devices: 16.4 us -> 6.13 us
  other arithmetic: 13.2 us -> 9.39 us
    all_gather x1 -> x0, waiting for transfers between devices: 82.9 us -> none  [side_by_side(): lax.all_gather(both, axis, axis=dim, tiled=True)]
    pallas_call x0 -> x1, Pallas kernels: none -> 65.9 us  [project(): pl.pallas_call(project_kernel, out_shape=(jax.ShapeDtypeStruct((tokens, c...]
    dot_general x2 -> x0, matrix products: 21.1 us -> none  [the longest x1 11.6 us: on_device(): raw_values = jnp.dot(hidden, pieces[1], preferred_element_type=jnp.float32)]
    all_to_all x1 -> x0, starting transfers between devices: 5.73 us -> none  [from_everyone(): lax.all_to_all(jnp.broadcast_to(shard[None], (devices, *shard.shape)), ax...]
    all_to_all x1, starting transfers between devices: 10.6 us -> 6.13 us  [on_device(): lax.all_to_all(outgoing.reshape((sources,) + outgoing.shape[2:]), ('seq',...]
    unnamed x15 -> x22, local copies, waits for them, and re-layouts: 2.07 us -> 5.01 us
  transfers between devices with their start and end apart: 3 -> 1, of which waited for: 2 -> 1; matrix products, arithmetic and copies ran while one was open for 9% -> 2% of each run, Pallas kernels for 0% -> 0%
where the time goes in v1:
time: 209 us; the launch traced here: 208 us
  waiting for transfers between devices  91.2 us (44%)
  Pallas kernels  65.9 us (32%)
  local copies, waits for them, and re-layouts  28.1 us (13%)
  other arithmetic  9.39 us (4%)
  starting transfers between devices  6.13 us (3%)
  blocking collectives  4.01 us (2%)
  matrix products  2.6 us (1%)
    all_to_all x1, waiting for transfers between devices, on_device(): lax.all_to_all(outgoing.reshape((sources,) + outgoing.shape[2:]), ('seq',...  91.2 us
    pallas_call x1, Pallas kernels, project(): pl.pallas_call(project_kernel, out_shape=(jax.ShapeDtypeStruct((tokens, c...  65.9 us
    gather x2, local copies, waits for them, and re-layouts, on_device(): received[slot_index].reshape(per_group, half_slots * PAGE, 2, columns)  7.6 us
    all_to_all x1, starting transfers between devices, on_device(): lax.all_to_all(outgoing.reshape((sources,) + outgoing.shape[2:]), ('seq',...  6.13 us
    slice x2, local copies, waits for them, and re-layouts, on_device(): cache_values = owned_pages[:, :, 1].reshape(per_group, -1, heads_kv, HD)  5.08 us
    unnamed x22, local copies, waits for them, and re-layouts  5.01 us
    select_n x1, other arithmetic, on_device(): jnp.where(send_live[..., None, None, None], page_pool[send_page], jnp.zer...  4.52 us
  transfers between devices with their start and end apart: 1, of which 1 were waited for; matrix products, arithmetic and copies ran while one was open for 2% of the time, Pallas kernels for 0%

profile of v1, /device:TPU:1, one launch (start us, length us, event | category | flops | bytes accessed | tf_op | source)
XLA Modules:
  0.0 208.4 jit_solution(8198001017801680668)
XLA Ops:
  0.7 0.8 add_select_fusion
  1.4 0.8 fusion.32
  2.2 0.1 copy.67
  2.4 0.1 eq.80
  2.5 0.1 eq.76
  2.6 0.8 lt.136
  3.4 0.1 lt.137
  3.5 0.1 lt.144
  3.6 0.1 lt.138
  3.7 0.1 copy.76
  3.8 0.1 broadcast_in_dim.131
  3.9 0.1 broadcast_in_dim.128
  4.0 0.1 lt.142
  4.1 1.2 reduce-window.6
  5.3 0.1 slice.101
  5.4 0.1 copy.71
  5.5 0.1 copy_bitcast_fusion
  5.7 0.1 lt.134
  5.8 0.2 fusion.14
  6.0 0.2 select_reduce_fusion
  6.2 0.1 copy.77
  6.3 0.2 reshape.552
  6.4 0.1 copy.74
  6.6 0.1 broadcast_in_dim.129
  6.7 0.1 copy.75
  6.8 0.8 copy-done
  7.6 0.8 copy-done.1
  8.5 0.7 copy-done.2
  9.2 65.9 %project.1 = (bf16[1024,256]{1,0:T(8,128)(2,1)S(1)}, bf16[1024,256]{1,0:T(8,128)(2,1)S(1)}, f32[1,256]{1,0:T(1,128)S(1)}) custom-call(bf16[1024,8192]{1,0:T(8,128)(2,1)} %hidden_hbm.1, bf16[128,256]{1,0:T(8,128)(2,1)S(1)} %copy-done, bf16[128,256]{1,0:T(8,128)(2,1)S(1)} %copy-done.1, f32[2,256]{1,0:T(2,128)S(1)} %copy-done.2), custom_call_target="tpu_custom_call" | custom-call | tf_op jit(solution)/shard_map/project/pallas_call | solution.py:288
  75.0 0.1 pad_maximum_fusion.1
  75.1 2.7 %gather_fusion = bf16[128,32,2,256]{3,1,2,0:T(8,128)(2,1)} fusion(bf16[32,32,2,256]{3,1,0,2:T(8,128)(2,1)S(1)} %pad_maximum_fusion.1, s32[1024]{0:T(1024)S(1)} %pad_clamp_fusion.1), kind=kCustom, calls=%fused_computation | custom fusion | bytes 8389120 | tf_op jit(solution)/shard_map/gather | solution.py:405
  77.9 4.5 %broadcast_select_fusion = bf16[64,2,32,2,256]{4,2,3,1,0:T(8,128)(2,1)} fusion(bf16[64,2,32,2,256]{4,2,3,1,0:T(8,128)(2,1)} %bitcast.92, pred[64,2]{1,0:T(8,128)(4,1)S(1)} %copy.75), kind=kLoop, calls=%fused_computation.2 | loop fusion | flops 2097152 | bytes 8388736 | tf_op jit(solution)/shard_map/jit(_where)/select_n | solution.py:404
  82.4 6.1 %all-to-all-start = ((bf16[64,2,32,2,256]{4,2,3,1,0:T(8,128)(2,1)}), bf16[64,2,32,2,256]{4,2,3,1,0:T(8,128)(2,1)}, u32[]{:S(2)}, u32[]{:S(2)}) async-start(bf16[64,2,32,2,256]{4,2,3,1,0:T(8,128)(2,1)} %broadcast_select_fusion), calls=%async_computation | async-start | bytes 8388608 | tf_op jit(solution)/shard_map/all_to_all | solution.py:407
  88.7 0.1 lt.152
  88.8 0.1 lt.154
  88.9 0.1 constant_dynamic-slice_fusion.1
  89.1 0.1 squeeze.7
  89.2 0.1 pad_maximum_fusion
  89.4 2.0 copy.90
  91.4 0.1 fusion.28
  91.5 0.2 reduce_window_sum.29
  91.8 0.1 add.152
  91.9 0.2 select_reduce_fusion.1
  92.2 0.7 fusion.58
  92.9 0.2 fusion.17
  93.2 91.2 %all-to-all-done = bf16[64,2,32,2,256]{4,2,3,1,0:T(8,128)(2,1)} async-done(((bf16[64,2,32,2,256]{4,2,3,1,0:T(8,128)(2,1)}), bf16[64,2,32,2,256]{4,2,3,1,0:T(8,128)(2,1)}, u32[]{:S(2)}, u32[]{:S(2)}) %all-to-all-start) | async-done | bytes 4194336 | tf_op jit(solution)/shard_map/all_to_all | solution.py:407
  184.4 5.0 %gather_fusion.1 = bf16[128,32,2,256]{3,1,2,0:T(8,128)(2,1)} fusion(bf16[128,32,2,256]{3,1,2,0:T(8,128)(2,1)} %bitcast.11, s32[1024]{0:T(1024)S(1)} %pad_clamp_fusion), kind=kCustom, calls=%fused_computation.1 | custom fusion | bytes 8389120 | tf_op jit(solution)/shard_map/gather | solution.py:433
  189.3 2.6 %copy.80 = bf16[128,32,2,256]{3,1,0,2:T(8,128)(2,1)S(1)} copy(bf16[128,32,2,256]{3,1,2,0:T(8,128)(2,1)} %gather_fusion.1) | data formatting | bytes 8388608 | tf_op jit(solution)/shard_map/gather | solution.py:433
  192.0 2.2 %fusion.54 = (bf16[8,512,1,256]{3,1,0,2:T(8,128)(2,1)}, bf16[8,512,1,256]{3,1,0,2:T(8,128)(2,1)}) fusion(bf16[8,512,2,256]{3,1,0,2:T(8,128)(2,1)S(1)} %bitcast.93), kind=kLoop, calls=%fused_computation.112 | loop fusion | bytes 8388608 | tf_op jit(solution)/shard_map/slice | solution.py:442
  194.2 2.9 %copy.81 = bf16[8,512,1,256]{1,3,0,2:T(8,128)(2,1)S(1)} copy(bf16[8,512,1,256]{3,1,0,2:T(8,128)(2,1)} %get-tuple-element.27) | data formatting | bytes 4194304 | tf_op jit(solution)/shard_map/slice | solution.py:441
  197.1 0.5 fusion.57
  197.6 0.1 reshape.545
  197.7 0.4 fusion.6
  198.1 0.1 reshape.546
  198.2 2.9 %copy.84 = bf16[8,512,1,256]{1,3,0,2:T(8,128)(2,1)S(1)} copy(bf16[8,512,1,256]{3,1,0,2:T(8,128)(2,1)} %get-tuple-element.26) | data formatting | bytes 4194304 | tf_op jit(solution)/shard_map/slice | solution.py:442
  201.1 0.8 fusion.8
  201.9 4.0 %all_to_all.10 = f32[2,520,128]{2,1,0:T(8,128)S(1)} all-to-all(f32[2,520,128]{2,1,0:T(8,128)S(1)} %broadcast_in_dim.138), channel_id=1, replica_groups=mesh['seq'=32,'head'=4,'rep'=2] {'rep'}, dimensions={0} | all-to-all | bytes 1064960 | tf_op jit(solution)/shard_map/all_to_all | solution.py:318
  205.9 0.1 slice.96
  206.1 0.1 slice.94
  206.2 0.1 slice.84
  206.3 0.1 slice.86
  206.5 0.6 fusion.4
  207.1 0.7 reshape.547
  207.8 0.6 copy.130
  (57 shorter events, 1.0 us)
Async XLA Ops:
  6.8 0.8 copy-start
  7.6 0.8 copy-start.1
  8.5 0.7 copy-start.2
  82.4 6.2 %copy-start.7 = (s32[256]{0:T(256)S(1)}, s32[256]{0:T(256)}, u32[]{:S(2)}) copy-start(s32[256]{0:T(256)} %param.15) | copy-start | bytes 3076
  82.4 6.5 %copy-start.4 = (s32[256,32]{0,1:T(8,128)S(1)}, s32[256,32]{0,1:T(8,128)}, u32[]{:S(2)}) copy-start(s32[256,32]{0,1:T(8,128)} %param.14) | copy-start | bytes 98308
  82.4 102.0 %all-to-all-start = ((bf16[64,2,32,2,256]{4,2,3,1,0:T(8,128)(2,1)}), bf16[64,2,32,2,256]{4,2,3,1,0:T(8,128)(2,1)}, u32[]{:S(2)}, u32[]{:S(2)}) async-start(bf16[64,2,32,2,256]{4,2,3,1,0:T(8,128)(2,1)} %broadcast_select_fusion), calls=%async_computation | async-start | bytes 8388608 | tf_op jit(solution)/shard_map/all_to_all | solution.py:407
  88.5 3.5 %copy-start.3 = (f32[2,256]{1,0:T(2,128)S(1)}, f32[2,256]{1,0:T(2,128)}, u32[]{:S(2)}) copy-start(f32[2,256]{1,0:T(2,128)} %scale_ref.1) | copy-start | bytes 6148
  88.5 3.6 %copy-start.6 = (bf16[4,8,2,256]{3,2,1,0:T(2,128)(2,1)S(1)}, bf16[4,8,2,256]{3,2,1,0:T(2,128)(2,1)}, u32[]{:S(2)}) copy-start(bf16[4,8,2,256]{3,2,1,0:T(2,128)(2,1)} %param.12) | copy-start | bytes 98308
  88.6 3.6 %copy-start.5 = (bf16[4,8,2048]{2,1,0:T(8,128)(2,1)S(1)}, bf16[4,8,2048]{2,1,0:T(8,128)(2,1)}, u32[]{:S(2)}) copy-start(bf16[4,8,2048]{2,1,0:T(8,128)(2,1)} %param.13) | copy-start | bytes 393220
  91.9 97.5 %copy-start.8 = (pred[4,4]{1,0:T(4,128)(4,1)}, pred[4,4]{1,0:T(4,128)(4,1)S(1)}, u32[]{:S(2)}) copy-start(pred[4,4]{1,0:T(4,128)(4,1)S(1)} %iota_compare_fusion.4) | copy-start | bytes 52
  201.0 5.4 %copy-start.9 = (pred[4,4]{1,0:T(4,128)(4,1)S(1)}, pred[4,4]{1,0:T(4,128)(4,1)}, u32[]{:S(2)}) copy-start(pred[4,4]{1,0:T(4,128)(4,1)} %copy-done.8) | copy-start | bytes 52

commit v2 on v1

v2 whole, which is shorter than its diff:
```python
import functools

import jax
import jax.numpy as jnp
from jax import lax
from jax.experimental import pallas as pl
from jax.experimental.pallas import tpu as pltpu
from jax.sharding import PartitionSpec as P

KVH = 8
HD = 128
QH = 64
PAGE = 32
NY = 4
NZ = 8
CHIPS = NY * NZ


EPSILON = 1e-05
NEGATIVE = -1e30


class Torus:
    def __init__(self):
        seq = lax.axis_index("seq")
        self.y, self.z = lax.div(seq, NZ), lax.rem(seq, NZ)
        self.core = lax.axis_index("rep")

    def at(self, dy, dz):
        y = lax.rem(self.y + (dy + NY), NY)
        z = lax.rem(self.z + (dz + NZ), NZ)
        return y * NZ + z


class Stream:
    def __init__(self, torus, number, block, send_sem, recv_sem, swap):
        self.torus, self.number, self.block = torus, number, block
        self.send_sem, self.recv_sem, self.swap = send_sem, recv_sem, swap

    def copy(self, blk, dy, dz):
        ref = self.block(blk, self.torus.core)
        return pltpu.make_async_remote_copy(
            src_ref=ref,
            dst_ref=ref,
            send_sem=self.send_sem,
            recv_sem=self.recv_sem.at[blk],
            device_id={"seq": self.torus.at(dy, dz)},
            device_id_type=pl.DeviceIdType.MESH,
        )

    def across(self, blk):
        if self.swap is None:
            return
        ref = self.block(blk, self.torus.core)
        pltpu.make_async_remote_copy(
            src_ref=ref,
            dst_ref=ref,
            send_sem=self.swap[0],
            recv_sem=self.swap[1],
            device_id={"rep": 1 - self.torus.core},
            device_id_type=pl.DeviceIdType.MESH,
        ).start()

    def arrived(self, dy, dz):
        blk = self.torus.at(dy, dz)
        self.copy(blk, 1, 0).wait_recv()
        return blk

    def along_z(self, blk, right, left):
        if right:
            self.copy(blk, 0, 1).start()
        if left:
            self.copy(blk, 0, -1).start()

    def along_y(self, blk, up, down):
        if up:
            self.copy(blk, 1, 0).start()
        if down:
            self.copy(blk, -1, 0).start()

    def step_z_first(self, st):
        turn_right = self.number % 2 == 0
        far = -4 if turn_right else 4
        reach = [[0], [-1, 1], [-2, 2], [-3, 3], [far]]
        if st == 0:
            blk = self.torus.at(0, 0)
            self.along_z(blk, True, True)
            self.along_y(blk, True, True)
            self.across(blk)
        if 1 <= st <= 4:
            for dz in reach[st]:
                blk = self.arrived(0, dz)
                onward = st < 3 or (st == 3 and (dz < 0) == turn_right)
                self.along_z(blk, onward and dz < 0, onward and dz > 0)
                self.along_y(blk, True, True)
                self.across(blk)
        if 1 <= st <= 5:
            for dz in reach[st - 1]:
                for dy in (-1, 1):
                    blk = self.arrived(dy, dz)
                    even = dz % 2 == 0
                    self.along_y(blk, even and dy < 0, not even and dy > 0)
                    self.across(blk)
        if 2 <= st <= 6:
            for dz in reach[st - 2]:
                self.across(self.arrived(2, dz))

    def step_y_first(self, st):
        even = self.number % 2 == 0
        if st == 0:
            blk = self.torus.at(0, 0)
            self.along_z(blk, True, True)
            self.along_y(blk, True, True)
            self.across(blk)
        if st == 1:
            for dy in (-1, 1):
                blk = self.arrived(dy, 0)
                self.along_y(blk, even and dy < 0, not even and dy > 0)
                self.along_z(blk, True, True)
                self.across(blk)
        if st == 2:
            blk = self.arrived(2, 0)
            self.along_z(blk, True, True)
            self.across(blk)
        for dy, first in ((0, 0), (-1, 1), (1, 1), (2, 2)):
            k = st - first
            turn_right = (self.number + dy) % 2 == 0
            if 1 <= k <= 3:
                for dz in (-k, k):
                    blk = self.arrived(dy, dz)
                    onward = k < 3 or (dz < 0) == turn_right
                    self.along_z(blk, onward and dz < 0, onward and dz > 0)
                    self.across(blk)
            if k == 4:
                self.across(self.arrived(dy, -4 if turn_right else 4))

    def step(self, st):
        @pl.when(self.torus.core == 0)
        def _():
            self.step_z_first(st)

        @pl.when(self.torus.core == 1)
        def _():
            self.step_y_first(st)

    def swap_copy(self, refs):
        return pltpu.make_async_remote_copy(
            src_ref=refs,
            dst_ref=refs,
            send_sem=self.swap[0],
            recv_sem=self.swap[1],
            device_id={"rep": 1 - self.torus.core},
            device_id_type=pl.DeviceIdType.MESH,
        )

    def sent_copy(self, refs):
        return pltpu.make_async_remote_copy(
            src_ref=refs,
            dst_ref=refs,
            send_sem=self.send_sem,
            recv_sem=self.recv_sem.at[0],
            device_id={"rep": 1 - self.torus.core},
            device_id_type=pl.DeviceIdType.MESH,
        )


STEPS_GATHER = 7
def greet(torus):
    barrier = pltpu.get_barrier_semaphore()
    for dy, dz in ((1, 0), (-1, 0), (0, 1), (0, -1)):
        pl.semaphore_signal(
            barrier,
            inc=1,
            device_id={"seq": torus.at(dy, dz)},
            device_id_type=pl.DeviceIdType.MESH,
        )
    pl.semaphore_signal(
        barrier,
        inc=1,
        device_id={"rep": 1 - torus.core},
        device_id_type=pl.DeviceIdType.MESH,
    )
    pl.semaphore_wait(barrier, 5)


SLOTS = 8


def find_kernel(table_ref, length_ref, found_ref):
    chip = lax.axis_index("seq")
    table = table_ref[...]
    slots, requests = table.shape
    slot = lax.broadcasted_iota(jnp.int32, table.shape, 0)
    lane = lax.broadcasted_iota(jnp.int32, table.shape, 1)
    left = length_ref[...] - slot * PAGE
    mine = ((left > 0) & (table // (2 * PAGE) == chip)).astype(jnp.float32)
    row = lax.broadcasted_iota(jnp.int32, (slots, slots), 0)
    column = lax.broadcasted_iota(jnp.int32, (slots, slots), 1)
    above = jnp.dot(
        (column < row).astype(jnp.float32), mine, preferred_element_type=jnp.float32
    )
    whole = jnp.broadcast_to(jnp.sum(mine, axis=0, keepdims=True), (8, requests))
    a = lax.broadcasted_iota(jnp.int32, (requests, requests), 0)
    b = lax.broadcasted_iota(jnp.int32, (requests, requests), 1)
    same = a // 8 == b // 8
    before = jnp.dot(
        whole, (same & (a < b)).astype(jnp.float32), preferred_element_type=jnp.float32
    )
    rank = jnp.where(mine > 0.0, above + before[0:1], -1.0)
    fields = (
        (lane % 8).astype(jnp.float32),
        (table % (2 * PAGE)).astype(jnp.float32),
        jnp.minimum(left, PAGE).astype(jnp.float32),
    )
    picked = jnp.concatenate(
        [
            jnp.sum(jnp.where(rank == e, field, 0.0), axis=0, keepdims=True)
            for field in fields
            for e in range(SLOTS)
        ],
        axis=0,
    )
    spread = jnp.dot(picked, same.astype(jnp.float32), preferred_element_type=jnp.float32)
    found_ref[...] = spread.astype(jnp.int32)


def find_pages(page_table, lengths):
    requests, slots = page_table.shape
    return pl.pallas_call(
        find_kernel,
        out_shape=jax.ShapeDtypeStruct((3 * SLOTS, requests), jnp.int32),
        name="find_pages",
    )(page_table.T, lengths.reshape(1, requests))


Y_AXIS, Z_AXIS = 0, 1


def below(keys, queries):
    return lax.dot_general(
        keys, queries, (((1,), (1,)), ((), ())), preferred_element_type=jnp.float32
    )


def weighed(values, weights):
    return lax.dot_general(
        values, weights, (((0,), (0,)), ((), ())), preferred_element_type=jnp.float32
    )


def attend(keys, values, queries, mask):
    scores = jnp.where(mask, below(keys, queries) * HD ** (-0.5), NEGATIVE)
    top = jnp.max(scores, axis=0, keepdims=True)
    weights = jnp.where(mask, jnp.exp(scores - top), 0.0)
    total = jnp.sum(weights, axis=0, keepdims=True)
    return top, total, weighed(values, weights.astype(jnp.bfloat16))


def fold(parts):
    top = functools.reduce(jnp.maximum, [p[0] for p in parts])
    scales = [jnp.exp(p[0] - top) for p in parts]
    total = functools.reduce(jnp.add, [p[1] * s for p, s in zip(parts, scales)])
    summed = functools.reduce(jnp.add, [p[2] * s for p, s in zip(parts, scales)])
    return top, total, summed


class Partials:
    def __init__(self, torus, part, stat, out, out_stat, got, got_stat, send_sem, recv_sem):
        self.torus, self.part, self.stat = torus, part, stat
        self.out, self.out_stat = out, out_stat
        self.got, self.got_stat = got, got_stat
        self.send_sem, self.recv_sem = send_sem, recv_sem

    def copies(self, g, axis, way):
        step = 1 - 2 * way
        peer = self.torus.at(step, 0) if axis == Y_AXIS else self.torus.at(0, step)
        return [
            pltpu.make_async_remote_copy(
                src_ref=src.at[g],
                dst_ref=dst.at[axis, way, g],
                send_sem=self.send_sem.at[k],
                recv_sem=self.recv_sem.at[k, axis, way, g],
                device_id={"seq": peer},
                device_id_type=pl.DeviceIdType.MESH,
            )
            for k, (src, dst) in enumerate(
                ((self.out, self.got), (self.out_stat, self.got_stat))
            )
        ]

    def gathered(self, g, arrivals, more=()):
        parts = [(self.stat[g, 0:1], self.stat[g, 1:2], self.part[g]), *more]
        for axis, way in arrivals:
            for copy in self.copies(g, axis, way):
                copy.wait_recv()
            stat = self.got_stat[axis, way, g]
            parts.append((stat[0:1], stat[1:2], self.got[axis, way, g].astype(jnp.float32)))
        return fold(parts) if len(parts) > 1 else parts[0]

    def send(self, dy, dz, arrivals, axis, way):
        g = self.torus.at(dy, dz)
        top, total, summed = self.gathered(g, arrivals)
        self.out[g] = summed.astype(jnp.bfloat16)
        self.out_stat[g] = jnp.concatenate([top, total], axis=0)
        for copy in self.copies(g, axis, way):
            copy.start()

    def y_first(self):
        order = (4, -3, 3, -2, 2, -1, 1, 0)
        up, down = (Y_AXIS, 0), (Y_AXIS, 1)
        for dz in order:
            self.send(2, dz, (), Y_AXIS, dz % 2)
        for dz in order:
            if dz % 2:
                self.send(1, dz, (), *up)
            else:
                self.send(-1, dz, (), *down)
        for dz in order:
            if dz % 2:
                self.send(-1, dz, (down,), *down)
            else:
                self.send(1, dz, (up,), *up)
        self.send(0, 4, (up, down), Z_AXIS, 0)
        self.send(0, -3, (up, down), Z_AXIS, 1)
        for dz in (3, -2, 2, -1, 1):
            way = 0 if dz > 0 else 1
            self.send(0, dz, (up, down, (Z_AXIS, way)), Z_AXIS, way)
    def z_first(self):
        right, left = (Z_AXIS, 0), (Z_AXIS, 1)
        rows = (2, 1, -1, 0)
        for dy in rows:
            self.send(dy, 4, (), Z_AXIS, dy % 2)
        for dy in rows:
            for dz in (3, -3) if dy % 2 else (-3, 3):
                way = 0 if dz > 0 else 1
                self.send(dy, dz, ((Z_AXIS, way),) if way == dy % 2 else (), Z_AXIS, way)
        for k in (2, 1):
            for dy in rows:
                self.send(dy, k, (right,), *right)
                self.send(dy, -k, (left,), *left)
        self.send(2, 0, (right, left), Y_AXIS, 0)
        self.send(-1, 0, (right, left), Y_AXIS, 1)
        self.send(1, 0, (right, left, (Y_AXIS, 0)), Y_AXIS, 0)


def decode_kernel(
    hidden_hbm, wk_hbm, wv_hbm, query_hbm, scale_ref, new_ref, found_ref,
    keys_ref, values_ref, smooth_ref, att_ref,
    hid, wk, wv, mx, qs, acc, kbuf, vbuf, kout, vout, part, stat, out, out_stat, got, got_stat,
    att_out,
    local_sem, hid_sem, send_sem, recv_sem, swap_sem, half_sem, part_send, part_recv,
):
    torus = Torus()
    me, core = torus.at(0, 0), torus.core
    tokens, depth = hidden_hbm.shape
    columns = wk_hbm.shape[1]
    steps_reqs = query_hbm.shape[0]
    half_q = query_hbm.shape[1] // 2
    heads = half_q // HD
    pages = tokens // PAGE
    parts = 4
    width = depth // parts
    own_k = pltpu.make_async_copy(wk_hbm, wk.at[me, core], local_sem.at[0])
    own_v = pltpu.make_async_copy(wv_hbm, wv.at[me, core], local_sem.at[1])
    own_q = pltpu.make_async_copy(
        query_hbm.at[:, pl.ds(pl.multiple_of(core * half_q, half_q), half_q)],
        qs.at[me],
        local_sem.at[2],
    )
    own_k.start()
    own_v.start()
    own_q.start()
    hid_copies = [
        pltpu.make_async_copy(
            hidden_hbm.at[:, pl.ds(k * width, width)],
            hid.at[:, pl.ds(k * width, width)],
            hid_sem.at[k],
        )
        for k in range(parts)
    ]
    for copy in hid_copies:
        copy.start()
    greet(torus)
    own_k.wait()

    def stream(number, block, swap=True):
        return Stream(
            torus,
            number,
            block,
            send_sem.at[number],
            recv_sem.at[number],
            (swap_sem.at[number, 0], swap_sem.at[number, 1]) if swap else None,
        )

    s_k = stream(0, lambda blk, c: wk.at[blk, c])
    s_v = stream(1, lambda blk, c: wv.at[blk, c])
    s_m = stream(2, lambda blk, c: mx.at[blk, c])
    s_q = stream(3, lambda blk, c: qs.at[blk], swap=False)
    rows = 512

    def multiply(weights, to, k):
        if k == 0:
            to[...] = jnp.zeros_like(to)
        blocks = weights.shape[0] // parts

        def one(m, carry):
            at = pl.ds(pl.multiple_of(m * rows, rows), rows)
            w = weights[k * blocks : (k + 1) * blocks].reshape(width, weights.shape[3])
            to[at, :] += jnp.dot(
                hid[at, k * width : (k + 1) * width], w, preferred_element_type=jnp.float32
            )
            return carry

        lax.fori_loop(0, tokens // rows, one, 0)

    mine = pl.ds(pl.multiple_of(core * HD, HD), HD)
    theirs = pl.ds(pl.multiple_of((1 - core) * HD, HD), HD)
    my_pages = pl.ds(pl.multiple_of(core * pages, pages), pages)
    their_pages = pl.ds(pl.multiple_of((1 - core) * pages, pages), pages)

    def half(k, leaving, whole, at):
        return pltpu.make_async_remote_copy(
            src_ref=leaving,
            dst_ref=whole.at[at],
            send_sem=half_sem.at[k, 0],
            recv_sem=half_sem.at[k, 1],
            device_id={"rep": 1 - core},
            device_id_type=pl.DeviceIdType.MESH,
        )

    def share(k, full, whole, leaving):
        leaving[...] = full[:, theirs].reshape(leaving.shape)
        whole[my_pages] = full[:, mine].reshape(leaving.shape)
        half(k, leaving, whole, my_pages).start()

    lag = {0: 0, 1: 3, 2: 9, 3: 6}
    for i in range(9 + STEPS_GATHER):
        if i == lag[1]:
            own_v.wait()
        if i == lag[3]:
            own_q.wait()
        for s in (s_k, s_v, s_q, s_m):
            st = i - lag[s.number]
            if 0 <= st < STEPS_GATHER:
                s.step(st)
        if i == 6:
            s_k.swap_copy(wk.at[:, 1 - core]).wait_recv()
        if i in (7, 8):
            for k in ((0, 1) if i == 7 else (2, 3)):
                hid_copies[k].wait()
                multiply(wk, acc.at[0], k)
        if i == 8:
            mx[me, core] = jnp.max(
                jnp.abs(acc[0]).reshape(tokens // 8, 8, columns), axis=0
            )
        if i == 9:
            s_v.swap_copy(wv.at[:, 1 - core]).wait_recv()
        if i in (10, 11, 12, 13):
            multiply(wv, acc.at[1], i - 10)
        if i == 14:
            values_ref[...] = jnp.clip(
                acc[1], -8.0 * scale_ref[1:2, :], 7.0 * scale_ref[1:2, :]
            ).astype(jnp.bfloat16)
            share(0, values_ref, vbuf, vout)
    s_m.swap_copy(mx.at[:, 1 - core]).wait_recv()
    peak = jnp.max(mx[...].reshape(2 * CHIPS, 8, columns), axis=0)
    smooth = jnp.sqrt(jnp.max(peak, axis=0, keepdims=True) + EPSILON)
    smooth_ref[...] = smooth
    keys_ref[...] = jnp.clip(
        acc[0] / smooth, -8.0 * scale_ref[0:1, :], 7.0 * scale_ref[0:1, :]
    ).astype(jnp.bfloat16)
    share(1, keys_ref, kbuf, kout)

    my_smooth = smooth_ref[:, mine]

    def queries_of(g):
        return jnp.concatenate(
            [
                (qs[g, :, h * HD : (h + 1) * HD].astype(jnp.float32) * my_smooth).astype(
                    jnp.bfloat16
                )
                for h in range(heads)
            ],
            axis=0,
        )

    across = heads * steps_reqs
    lane = lax.broadcasted_iota(jnp.int32, (PAGE, across), 1)
    key = lax.broadcasted_iota(jnp.int32, (PAGE, across), 0)
    request = lane % 8

    fresh_keys = jnp.clip(
        new_ref[:, mine].astype(jnp.float32) / my_smooth,
        -8.0 * scale_ref[0:1, mine],
        7.0 * scale_ref[0:1, mine],
    ).astype(jnp.bfloat16)
    fresh_values = jnp.clip(
        new_ref[:, pl.ds(pl.multiple_of(columns + core * HD, HD), HD)].astype(jnp.float32),
        -8.0 * scale_ref[1:2, mine],
        7.0 * scale_ref[1:2, mine],
    ).astype(jnp.bfloat16)
    fresh_mask = (key % 8 == request) & (key // 8 <= (lane // 8) % (steps_reqs // 8))
    fresh = attend(fresh_keys, fresh_values, queries_of(me), fresh_mask)

    half(0, vout, vbuf, their_pages).wait_recv()
    half(1, kout, kbuf, their_pages).wait_recv()

    def one_group(g):
        keys, values, masks = [], [], []
        for e in range(SLOTS):
            who, page, count = (found_ref[SLOTS * f + e, g * 8] for f in range(3))
            keys.append(kbuf[page])
            values.append(vbuf[page])
            masks.append((request == who) & (key < count))
        top, total, summed = attend(
            jnp.concatenate(keys, axis=0),
            jnp.concatenate(values, axis=0),
            queries_of(g),
            jnp.concatenate(masks, axis=0),
        )
        part[g] = summed
        stat[g] = jnp.concatenate([top, total], axis=0)

    def groups(i, carry):
        one_group(2 * i)
        one_group(2 * i + 1)
        return carry

    lax.fori_loop(0, CHIPS // 2, groups, 0)

    partials = Partials(
        torus, part, stat, out, out_stat, got, got_stat, part_send, part_recv
    )

    @pl.when(core == 0)
    def _():
        partials.y_first()

    @pl.when(core == 1)
    def _():
        partials.z_first()

    top, total, summed = partials.gathered(
        me, ((Y_AXIS, 0), (Y_AXIS, 1), (Z_AXIS, 0), (Z_AXIS, 1)), more=(fresh,)
    )
    done = (summed / total).T.astype(jnp.bfloat16)
    for h in range(heads):
        att_out[:, h * HD : (h + 1) * HD] = done[h * steps_reqs : (h + 1) * steps_reqs]
    own_att = pl.ds(pl.multiple_of(core * half_q, half_q), half_q)
    last = pltpu.make_async_remote_copy(
        src_ref=att_out,
        dst_ref=att_ref.at[:, own_att],
        send_sem=half_sem.at[2, 0],
        recv_sem=half_sem.at[2, 1],
        device_id={"rep": 1 - core},
        device_id_type=pl.DeviceIdType.MESH,
    )
    last.start()
    att_ref[:, own_att] = att_out[...]

    for s, refs in ((s_k, wk), (s_v, wv), (s_m, mx)):
        s.sent_copy(refs.at[pl.ds(0, CHIPS - 1), core]).wait_send()
        s.swap_copy(refs.at[:, core]).wait_send()
    s_q.sent_copy(qs.at[pl.ds(0, CHIPS - 1)]).wait_send()
    half(0, vout, vbuf, my_pages).wait_send()
    half(1, kout, kbuf, my_pages).wait_send()
    for k, refs in enumerate((out, out_stat)):
        pltpu.make_async_remote_copy(
            src_ref=refs.at[pl.ds(0, CHIPS - 1)],
            dst_ref=refs.at[pl.ds(0, CHIPS - 1)],
            send_sem=part_send.at[k],
            recv_sem=part_recv.at[k, 0, 0, 0],
            device_id={"rep": 1 - core},
            device_id_type=pl.DeviceIdType.MESH,
        ).wait_send()
    last.wait()


def decode(hidden, key_weight, value_weight, queries, group_scale, new_kv, found):
    tokens, depth = hidden.shape
    rows, columns = key_weight.shape
    step_reqs, q_columns = queries.shape
    pages = tokens // PAGE
    across = q_columns // 2 // HD * step_reqs
    bf16, f32 = jnp.bfloat16, jnp.float32
    any_spec = pl.BlockSpec(memory_space=pl.ANY)
    vmem = pl.BlockSpec(memory_space=pltpu.VMEM)
    smem = pl.BlockSpec(memory_space=pltpu.SMEM)
    return pl.pallas_call(
        decode_kernel,
        out_shape=(
            jax.ShapeDtypeStruct((tokens, columns), bf16),
            jax.ShapeDtypeStruct((tokens, columns), bf16),
            jax.ShapeDtypeStruct((1, columns), f32),
            jax.ShapeDtypeStruct((step_reqs, q_columns), bf16),
        ),
        in_specs=[any_spec, any_spec, any_spec, any_spec, vmem, vmem, smem],
        out_specs=(vmem, vmem, vmem, vmem),
        scratch_shapes=[
            pltpu.VMEM((tokens, depth), bf16),
            pltpu.VMEM((CHIPS, 2, rows, columns), bf16),
            pltpu.VMEM((CHIPS, 2, rows, columns), bf16),
            pltpu.VMEM((CHIPS, 2, 8, columns), f32),
            pltpu.VMEM((CHIPS, step_reqs, q_columns // 2), bf16),
            pltpu.VMEM((2, tokens, columns), f32),
            pltpu.VMEM((2 * pages, PAGE, HD), bf16),
            pltpu.VMEM((2 * pages, PAGE, HD), bf16),
            pltpu.VMEM((pages, PAGE, HD), bf16),
            pltpu.VMEM((pages, PAGE, HD), bf16),
            pltpu.VMEM((CHIPS, HD, across), f32),
            pltpu.VMEM((CHIPS, 2, across), f32),
            pltpu.VMEM((CHIPS, HD, across), bf16),
            pltpu.VMEM((CHIPS, 2, across), f32),
            pltpu.VMEM((2, 2, CHIPS, HD, across), bf16),
            pltpu.VMEM((2, 2, CHIPS, 2, across), f32),
            pltpu.VMEM((step_reqs, q_columns // 2), bf16),
            pltpu.SemaphoreType.DMA((3,)),
            pltpu.SemaphoreType.DMA((4,)),
            pltpu.SemaphoreType.DMA((4,)),
            pltpu.SemaphoreType.DMA((4, CHIPS)),
            pltpu.SemaphoreType.DMA((3, 2)),
            pltpu.SemaphoreType.DMA((3, 2)),
            pltpu.SemaphoreType.DMA((2,)),
            pltpu.SemaphoreType.DMA((2, 2, 2, CHIPS)),
        ],
        compiler_params=pltpu.CompilerParams(
            collective_id=0, has_side_effects=True, vmem_limit_bytes=60 * 2**20
        ),
        name="decode",
    )(hidden, key_weight, value_weight, queries, group_scale, new_kv, found)


def on_device(
    hidden, key_weight, value_weight, group_scale, new_kv, decode_query, page_table, lengths
):
    steps, requests, q_columns = decode_query.shape
    columns = key_weight.shape[1]
    found = find_pages(page_table, lengths)
    keys, values, smoothing, attention = decode(
        hidden,
        key_weight,
        value_weight,
        decode_query.reshape(steps * requests, q_columns),
        group_scale,
        new_kv.reshape(steps * requests, 2 * columns),
        found,
    )
    kv_cache = jnp.stack([keys, values], axis=1)
    return (
        kv_cache,
        smoothing.reshape(columns),
        attention.reshape(steps, requests, q_columns),
    )


def solution(mesh):
    placed = (
        P(("seq", "rep"), None),
        P(("seq", "rep"), "head"),
        P(("seq", "rep"), "head"),
        P(None, "head"),
        P(None, "seq", None, "head"),
        P(None, "seq", "head"),
        P(),
        P(),
    )
    return jax.shard_map(
        on_device,
        mesh=mesh,
        in_specs=placed,
        out_specs=(P(("seq", "rep"), None, "head"), P("head"), P(None, "seq", "head")),
        check_vma=False,
    )
```

time: 209 us -> 127 us (0.61)
  waiting for transfers between devices: 91.2 us -> 0 us
  Pallas kernels: 65.9 us -> 119 us
  local copies, waits for them, and re-layouts: 28.1 us -> 6.21 us
  other arithmetic: 9.39 us -> 1.3 us
  starting transfers between devices: 6.13 us -> 0 us
  blocking collectives: 4.01 us -> 0 us
  matrix products: 2.6 us -> 0 us
    all_to_all x1 -> x0, waiting for transfers between devices: 91.2 us -> none  [on_device(): lax.all_to_all(outgoing.reshape((sources,) + outgoing.shape[2:]), ('seq',...]
    pallas_call x1 -> x2, Pallas kernels: 65.9 us -> 119 us  [the longest x1 117 us: decode(): pl.pallas_call(decode_kernel, out_shape=(jax.ShapeDtypeStruct((tokens, co...]
    gather x3 -> x0, local copies, waits for them, and re-layouts: 10.3 us -> none  [the longest x2 7.6 us: on_device(): received[slot_index].reshape(per_group, half_slots * PAGE, 2, columns)]
    slice x11 -> x0, local copies, waits for them, and re-layouts: 8.56 us -> none  [the longest x2 5.08 us: on_device(): cache_values = owned_pages[:, :, 1].reshape(per_group, -1, heads_kv, HD)]
    all_to_all x1 -> x0, starting transfers between devices: 6.13 us -> none  [on_device(): lax.all_to_all(outgoing.reshape((sources,) + outgoing.shape[2:]), ('seq',...]
    select_n x6 -> x0, other arithmetic: 5.33 us -> none  [the longest x1 4.52 us: on_device(): jnp.where(send_live[..., None, None, None], page_pool[send_page], jnp.zer...]
    all_to_all x1 -> x0, blocking collectives: 4.01 us -> none  [from_everyone(): lax.all_to_all(jnp.broadcast_to(shard[None], (devices, *shard.shape)), ax...]
    dot_general x4 -> x0, matrix products: 2.6 us -> none  [the longest x1 0.8 us: on_device(): jnp.einsum('rktgn,rnkd->rktgd', weights.astype(jnp.bfloat16), cache_value...]
  transfers between devices with their start and end apart: 1 -> 0, of which waited for: 1 -> 0; matrix products, arithmetic and copies ran while one was open for 2% -> 0% of each run, Pallas kernels for 0% -> 0%
where the time goes in v2:
time: 127 us
  Pallas kernels  119 us (94%)
  local copies, waits for them, and re-layouts  6.21 us (5%)
  other arithmetic  1.3 us (1%)
    pallas_call x1, Pallas kernels, decode(): pl.pallas_call(decode_kernel, out_shape=(jax.ShapeDtypeStruct((tokens, co...  117 us
    unnamed x4, local copies, waits for them, and re-layouts  6.21 us

profile of v2, /device:TPU:1, one launch (start us, length us, event | category | flops | bytes accessed | tf_op | source)
XLA Modules:
  0.0 126.9 jit_solution(9806802435691410988)
XLA Ops:
  0.6 1.8 %find_pages.1.found_ref = s32[24,256]{1,0:T(8,128)} custom-call(s32[32,256]{1,0:T(8,128)} %bitcast.15, s32[1,256]{1,0:T(1,128)} %bitcast.16), custom_call_target="tpu_custom_call" | custom-call | tf_op jit(solution)/shard_map/find_pages/pallas_call | solution.py:229
  2.4 1.4 %copy.12 = bf16[4,8,2,256]{3,1,2,0:T(8,128)(2,1)} copy(bf16[4,8,2,256]{3,2,1,0:T(2,128)(2,1)} %param.12) | data formatting | bytes 65536
  3.8 116.9 %decode.1 = (bf16[1024,256]{1,0:T(8,128)(2,1)}, bf16[1024,256]{1,0:T(8,128)(2,1)}, f32[1,256]{1,0:T(1,128)}, bf16[32,2048]{1,0:T(8,128)(2,1)}) custom-call(bf16[1024,8192]{1,0:T(8,128)(2,1)} %hidden_hbm.1, bf16[128,256]{1,0:T(8,128)(2,1)} %wk_hbm.1, bf16[128,256]{1,0:T(8,128)(2,1)} %wv_hbm.1, bf16[32,2048]{1,0:T(8,128)(2,1)} %bitcast.12, ...), custom_call_target="tpu_custom_call" | custom-call | tf_op jit(solution)/shard_map/decode/pallas_call | solution.py:590
  120.7 1.3 %pad_maximum_fusion = bf16[1024,2,256]{2,0,1:T(8,128)(2,1)S(1)} fusion(bf16[1024,1,256]{2,0,1:T(8,128)(2,1)} %bitcast.11, bf16[1024,1,256]{2,0,1:T(8,128)(2,1)} %bitcast.10), kind=kLoop, calls=%fused_computation | loop fusion | flops 524288 | bytes 2097152 | tf_op jit(solution)/shard_map/stack | solution.py:649
  122.0 2.0 %copy.11 = bf16[1024,2,256]{2,1,0:T(2,128)(2,1)} copy(bf16[1024,2,256]{2,0,1:T(8,128)(2,1)S(1)} %pad_maximum_fusion) | data formatting | bytes 2097152
  124.1 1.2 copy.15
  125.3 1.6 %copy.16 = bf16[4,8,2048]{2,1,0:T(8,128)(2,1)} copy(bf16[4,8,2048]{2,1,0:T(8,128)(2,1)} %bitcast.14) | data formatting | bytes 262144

commit v3 on v2

--- a/solution.py
+++ b/solution.py
@@ -33,8 +33,8 @@
 
 
 class Stream:
-    def __init__(self, torus, number, block, send_sem, recv_sem, swap):
-        self.torus, self.number, self.block = torus, number, block
+    def __init__(self, torus, number, block, send_sem, recv_sem, swap, both_z=False):
+        self.torus, self.number, self.block, self.both_z = torus, number, block, both_z
         self.send_sem, self.recv_sem, self.swap = send_sem, recv_sem, swap
 
     def copy(self, blk, dy, dz):
@@ -56,7 +56,7 @@
             src_ref=ref,
             dst_ref=ref,
             send_sem=self.swap[0],
-            recv_sem=self.swap[1],
+            recv_sem=self.swap[1].at[lax.div(blk, NZ)],
             device_id={"rep": 1 - self.torus.core},
             device_id_type=pl.DeviceIdType.MESH,
         ).start()
@@ -135,6 +135,10 @@
                 self.across(self.arrived(dy, -4 if turn_right else 4))
 
     def step(self, st):
+        if self.both_z:
+            self.step_z_first(st)
+            return
+
         @pl.when(self.torus.core == 0)
         def _():
             self.step_z_first(st)
@@ -143,12 +147,12 @@
         def _():
             self.step_y_first(st)
 
-    def swap_copy(self, refs):
+    def swap_copy(self, refs, row=0):
         return pltpu.make_async_remote_copy(
             src_ref=refs,
             dst_ref=refs,
             send_sem=self.swap[0],
-            recv_sem=self.swap[1],
+            recv_sem=self.swap[1].at[row],
             device_id={"rep": 1 - self.torus.core},
             device_id_type=pl.DeviceIdType.MESH,
         )
@@ -165,22 +169,24 @@
 
 
 STEPS_GATHER = 7
+QUERY_LAG = 3
+def friends(torus):
+    ring = [(torus.at(0, dz), torus.core) for dz in (1, -1, 2, -2, 3, -3, 4)]
+    ring += [(torus.at(0, dz), 1 - torus.core) for dz in (0, 1, -1, 2, -2, 3, -3, 4)]
+    return ring, [(torus.at(dy, 0), torus.core) for dy in (1, -1, 2)]
+
+
 def greet(torus):
     barrier = pltpu.get_barrier_semaphore()
-    for dy, dz in ((1, 0), (-1, 0), (0, 1), (0, -1)):
+    ring, column = friends(torus)
+    for place, core in ring + column:
         pl.semaphore_signal(
             barrier,
             inc=1,
-            device_id={"seq": torus.at(dy, dz)},
+            device_id={"seq": place, "rep": core},
             device_id_type=pl.DeviceIdType.MESH,
         )
-    pl.semaphore_signal(
-        barrier,
-        inc=1,
-        device_id={"rep": 1 - torus.core},
-        device_id_type=pl.DeviceIdType.MESH,
-    )
-    pl.semaphore_wait(barrier, 5)
+    pl.semaphore_wait(barrier, len(ring) + len(column))
 
 
 SLOTS = 8
@@ -305,39 +311,64 @@
         for copy in self.copies(g, axis, way):
             copy.start()
 
-    def y_first(self):
+    def y_first(self, attend_to):
         order = (4, -3, 3, -2, 2, -1, 1, 0)
         up, down = (Y_AXIS, 0), (Y_AXIS, 1)
+
+        def row(dy):
+            attend_to(NZ, lambda k: self.torus.at(dy, 4 - k))
+
+        row(2)
         for dz in order:
             self.send(2, dz, (), Y_AXIS, dz % 2)
+        row(1)
         for dz in order:
             if dz % 2:
                 self.send(1, dz, (), *up)
-            else:
+        row(-1)
+        for dz in order:
+            if dz % 2 == 0:
                 self.send(-1, dz, (), *down)
         for dz in order:
             if dz % 2:
                 self.send(-1, dz, (down,), *down)
             else:
                 self.send(1, dz, (up,), *up)
+        row(0)
         self.send(0, 4, (up, down), Z_AXIS, 0)
         self.send(0, -3, (up, down), Z_AXIS, 1)
         for dz in (3, -2, 2, -1, 1):
             way = 0 if dz > 0 else 1
             self.send(0, dz, (up, down, (Z_AXIS, way)), Z_AXIS, way)
-    def z_first(self):
+
+    def z_first(self, attend_to):
         right, left = (Z_AXIS, 0), (Z_AXIS, 1)
         rows = (2, 1, -1, 0)
+
+        def columns(dz, count):
+            attend_to(
+                count,
+                lambda k: self.torus.at(
+                    2 - lax.rem(k, NY), dz * (1 - 2 * lax.div(k, NY)) if dz else 0
+                ),
+            )
+
+        columns(4, NY)
         for dy in rows:
             self.send(dy, 4, (), Z_AXIS, dy % 2)
+        columns(3, 2 * NY)
         for dy in rows:
-            for dz in (3, -3) if dy % 2 else (-3, 3):
-                way = 0 if dz > 0 else 1
-                self.send(dy, dz, ((Z_AXIS, way),) if way == dy % 2 else (), Z_AXIS, way)
-        for k in (2, 1):
+            way = 1 - dy % 2
+            self.send(dy, -3 if way else 3, (), Z_AXIS, way)
+        for dy in rows:
+            way = dy % 2
+            self.send(dy, -3 if way else 3, ((Z_AXIS, way),), Z_AXIS, way)
+        for dz in (2, 1):
+            columns(dz, 2 * NY)
             for dy in rows:
-                self.send(dy, k, (right,), *right)
-                self.send(dy, -k, (left,), *left)
+                self.send(dy, dz, (right,), *right)
+                self.send(dy, -dz, (left,), *left)
+        columns(0, NY)
         self.send(2, 0, (right, left), Y_AXIS, 0)
         self.send(-1, 0, (right, left), Y_AXIS, 1)
         self.send(1, 0, (right, left, (Y_AXIS, 0)), Y_AXIS, 0)
@@ -346,9 +377,10 @@
 def decode_kernel(
     hidden_hbm, wk_hbm, wv_hbm, query_hbm, scale_ref, new_ref, found_ref,
     keys_ref, values_ref, smooth_ref, att_ref,
-    hid, wk, wv, mx, qs, acc, kbuf, vbuf, kout, vout, part, stat, out, out_stat, got, got_stat,
+    hid, wk, wv, mz, my, qs, acc, kbuf, vbuf, kout, vout, part, stat, out, out_stat, got, got_stat,
     att_out,
-    local_sem, hid_sem, send_sem, recv_sem, swap_sem, half_sem, part_send, part_recv,
+    local_sem, hid_sem, send_sem, recv_sem, swap_send, swap_recv, peak_sem, half_sem,
+    part_send, part_recv,
 ):
     torus = Torus()
     me, core = torus.at(0, 0), torus.core
@@ -362,14 +394,21 @@
     width = depth // parts
     own_k = pltpu.make_async_copy(wk_hbm, wk.at[me, core], local_sem.at[0])
     own_v = pltpu.make_async_copy(wv_hbm, wv.at[me, core], local_sem.at[1])
-    own_q = pltpu.make_async_copy(
-        query_hbm.at[:, pl.ds(pl.multiple_of(core * half_q, half_q), half_q)],
-        qs.at[me],
-        local_sem.at[2],
-    )
+    own_q = [
+        pltpu.make_async_copy(
+            query_hbm.at[
+                pl.ds(k * (steps_reqs // 2), steps_reqs // 2),
+                pl.ds(pl.multiple_of(core * half_q, half_q), half_q),
+            ],
+            qs.at[me, k],
+            local_sem.at[2 + k],
+        )
+        for k in range(2)
+    ]
     own_k.start()
     own_v.start()
-    own_q.start()
+    for copy in own_q:
+        copy.start()
     hid_copies = [
         pltpu.make_async_copy(
             hidden_hbm.at[:, pl.ds(k * width, width)],
@@ -383,33 +422,37 @@
     greet(torus)
     own_k.wait()
 
-    def stream(number, block, swap=True):
+    def stream(number, block, swap=True, both_z=False):
         return Stream(
             torus,
             number,
             block,
             send_sem.at[number],
             recv_sem.at[number],
-            (swap_sem.at[number, 0], swap_sem.at[number, 1]) if swap else None,
+            (swap_send.at[number], swap_recv.at[number]) if swap else None,
+            both_z,
         )
 
     s_k = stream(0, lambda blk, c: wk.at[blk, c])
     s_v = stream(1, lambda blk, c: wv.at[blk, c])
-    s_m = stream(2, lambda blk, c: mx.at[blk, c])
-    s_q = stream(3, lambda blk, c: qs.at[blk], swap=False)
+    s_qa = stream(2, lambda blk, c: qs.at[blk, 0], swap=False)
+    s_qb = stream(3, lambda blk, c: qs.at[blk, 1], swap=False, both_z=True)
     rows = 512
 
-    def multiply(weights, to, k):
-        if k == 0:
-            to[...] = jnp.zeros_like(to)
-        blocks = weights.shape[0] // parts
+    def multiply(stream, weights, to, dy):
+        y = lax.rem(torus.y + (dy + NY), NY)
+        blocks = pl.ds(pl.multiple_of(y * NZ, NZ), NZ)
+        stream.swap_copy(weights.at[blocks, 1 - core], y).wait_recv()
 
         def one(m, carry):
             at = pl.ds(pl.multiple_of(m * rows, rows), rows)
-            w = weights[k * blocks : (k + 1) * blocks].reshape(width, weights.shape[3])
-            to[at, :] += jnp.dot(
-                hid[at, k * width : (k + 1) * width], w, preferred_element_type=jnp.float32
+            w = weights[blocks].reshape(width, weights.shape[3])
+            product = jnp.dot(
+                hid[at, pl.ds(pl.multiple_of(y * width, width), width)],
+                w,
+                preferred_element_type=jnp.float32,
             )
+            to[at, :] = product if dy == 0 else to[at, :] + product
             return carry
 
         lax.fori_loop(0, tokens // rows, one, 0)
@@ -434,37 +477,62 @@
         whole[my_pages] = full[:, mine].reshape(leaving.shape)
         half(k, leaving, whole, my_pages).start()
 
-    lag = {0: 0, 1: 3, 2: 9, 3: 6}
-    for i in range(9 + STEPS_GATHER):
-        if i == lag[1]:
+    ring, column = friends(torus)
+    place = core * NZ + torus.z
+
+    def peak_copy(refs, slot, k, target):
+        return pltpu.make_async_remote_copy(
+            src_ref=refs.at[slot],
+            dst_ref=refs.at[slot],
+            send_sem=peak_sem.at[k, 0],
+            recv_sem=peak_sem.at[k, 1],
+            device_id={"seq": target[0], "rep": target[1]},
+            device_id_type=pl.DeviceIdType.MESH,
+        )
+
+    def tell(refs, slot, k, peers):
+        for target in peers:
+            peak_copy(refs, slot, k, target).start()
+
+    def heard(refs, k, peers):
+        return peak_copy(refs, pl.ds(0, len(peers)), k, peers[0])
+
+    q_lag = QUERY_LAG
+    for i in range(q_lag + STEPS_GATHER):
+        if i == 0:
             own_v.wait()
-        if i == lag[3]:
-            own_q.wait()
-        for s in (s_k, s_v, s_q, s_m):
-            st = i - lag[s.number]
-            if 0 <= st < STEPS_GATHER:
-                s.step(st)
+        if i == q_lag:
+            for copy in own_q:
+                copy.wait()
+        for stream_i, start in ((s_k, 0), (s_v, 0), (s_qa, q_lag), (s_qb, q_lag)):
+            if 0 <= i - start < STEPS_GATHER:
+                stream_i.step(i - start)
+        if i == 5:
+            for copy in hid_copies:
+                copy.wait()
+            multiply(s_k, wk, acc.at[0], 0)
+            multiply(s_v, wv, acc.at[1], 0)
         if i == 6:
-            s_k.swap_copy(wk.at[:, 1 - core]).wait_recv()
-        if i in (7, 8):
-            for k in ((0, 1) if i == 7 else (2, 3)):
-                hid_copies[k].wait()
-                multiply(wk, acc.at[0], k)
+            multiply(s_k, wk, acc.at[0], 1)
+            multiply(s_k, wk, acc.at[0], -1)
+            multiply(s_k, wk, acc.at[0], 2)
+            mz[place] = jnp.max(jnp.abs(acc[0]).reshape(tokens // 8, 8, columns), axis=0)
+            tell(mz, place, 0, ring)
+        if i == 7:
+            multiply(s_v, wv, acc.at[1], 1)
+            multiply(s_v, wv, acc.at[1], -1)
         if i == 8:
-            mx[me, core] = jnp.max(
-                jnp.abs(acc[0]).reshape(tokens // 8, 8, columns), axis=0
-            )
+            heard(mz, 0, ring).wait_recv()
+            my[torus.y] = jnp.max(mz[...], axis=0)
+            tell(my, torus.y, 1, column)
+            multiply(s_v, wv, acc.at[1], 2)
         if i == 9:
-            s_v.swap_copy(wv.at[:, 1 - core]).wait_recv()
-        if i in (10, 11, 12, 13):
-            multiply(wv, acc.at[1], i - 10)
-        if i == 14:
             values_ref[...] = jnp.clip(
                 acc[1], -8.0 * scale_ref[1:2, :], 7.0 * scale_ref[1:2, :]
             ).astype(jnp.bfloat16)
             share(0, values_ref, vbuf, vout)
-    s_m.swap_copy(mx.at[:, 1 - core]).wait_recv()
-    peak = jnp.max(mx[...].reshape(2 * CHIPS, 8, columns), axis=0)
+    heard(my, 1, column).wait_recv()
+    peak = jnp.max(my[...], axis=0)
     smooth = jnp.sqrt(jnp.max(peak, axis=0, keepdims=True) + EPSILON)
     smooth_ref[...] = smooth
     keys_ref[...] = jnp.clip(
@@ -477,9 +545,12 @@
     def queries_of(g):
         return jnp.concatenate(
             [
-                (qs[g, :, h * HD : (h + 1) * HD].astype(jnp.float32) * my_smooth).astype(
-                    jnp.bfloat16
-                )
+                (
+                    qs[g, :, :, h * HD : (h + 1) * HD]
+                    .reshape(steps_reqs, HD)
+                    .astype(jnp.float32)
+                    * my_smooth
+                ).astype(jnp.bfloat16)
                 for h in range(heads)
             ],
             axis=0,
@@ -522,12 +593,13 @@
         part[g] = summed
         stat[g] = jnp.concatenate([top, total], axis=0)
 
-    def groups(i, carry):
-        one_group(2 * i)
-        one_group(2 * i + 1)
-        return carry
-
-    lax.fori_loop(0, CHIPS // 2, groups, 0)
+    def attend_to(count, group):
+        def two(i, carry):
+            one_group(group(2 * i))
+            one_group(group(2 * i + 1))
+            return carry
+
+        lax.fori_loop(0, count // 2, two, 0)
 
     partials = Partials(
         torus, part, stat, out, out_stat, got, got_stat, part_send, part_recv
@@ -535,11 +607,11 @@
 
     @pl.when(core == 0)
     def _():
-        partials.y_first()
+        partials.y_first(attend_to)
 
     @pl.when(core == 1)
     def _():
-        partials.z_first()
+        partials.z_first(attend_to)
 
     top, total, summed = partials.gathered(
         me, ((Y_AXIS, 0), (Y_AXIS, 1), (Z_AXIS, 0), (Z_AXIS, 1)), more=(fresh,)
@@ -559,10 +631,13 @@
     last.start()
     att_ref[:, own_att] = att_out[...]
 
-    for s, refs in ((s_k, wk), (s_v, wv), (s_m, mx)):
+    for s, refs in ((s_k, wk), (s_v, wv)):
         s.sent_copy(refs.at[pl.ds(0, CHIPS - 1), core]).wait_send()
         s.swap_copy(refs.at[:, core]).wait_send()
-    s_q.sent_copy(qs.at[pl.ds(0, CHIPS - 1)]).wait_send()
+    s_qa.sent_copy(qs.at[pl.ds(0, CHIPS - 1), 0]).wait_send()
+    s_qb.sent_copy(qs.at[pl.ds(0, CHIPS - 1), 1]).wait_send()
+    heard(mz, 0, ring).wait_send()
+    heard(my, 1, column).wait_send()
     half(0, vout, vbuf, my_pages).wait_send()
     half(1, kout, kbuf, my_pages).wait_send()
     for k, refs in enumerate((out, out_stat)):
@@ -601,8 +676,9 @@
             pltpu.VMEM((tokens, depth), bf16),
             pltpu.VMEM((CHIPS, 2, rows, columns), bf16),
             pltpu.VMEM((CHIPS, 2, rows, columns), bf16),
-            pltpu.VMEM((CHIPS, 2, 8, columns), f32),
-            pltpu.VMEM((CHIPS, step_reqs, q_columns // 2), bf16),
+            pltpu.VMEM((2 * NZ, 8, columns), f32),
+            pltpu.VMEM((NY, 8, columns), f32),
+            pltpu.VMEM((CHIPS, 2, step_reqs // 2, q_columns // 2), bf16),
             pltpu.VMEM((2, tokens, columns), f32),
             pltpu.VMEM((2 * pages, PAGE, HD), bf16),
             pltpu.VMEM((2 * pages, PAGE, HD), bf16),
@@ -615,11 +691,13 @@
             pltpu.VMEM((2, 2, CHIPS, HD, across), bf16),
             pltpu.VMEM((2, 2, CHIPS, 2, across), f32),
             pltpu.VMEM((step_reqs, q_columns // 2), bf16),
-            pltpu.SemaphoreType.DMA((3,)),
+            pltpu.SemaphoreType.DMA((4,)),
             pltpu.SemaphoreType.DMA((4,)),
             pltpu.SemaphoreType.DMA((4,)),
             pltpu.SemaphoreType.DMA((4, CHIPS)),
-            pltpu.SemaphoreType.DMA((3, 2)),
+            pltpu.SemaphoreType.DMA((2,)),
+            pltpu.SemaphoreType.DMA((2, NY)),
+            pltpu.SemaphoreType.DMA((2, 2)),
             pltpu.SemaphoreType.DMA((3, 2)),
             pltpu.SemaphoreType.DMA((2,)),
             pltpu.SemaphoreType.DMA((2, 2, 2, CHIPS)),
@@ -629,6 +707,40 @@
         ),
         name="decode",
     )(hidden, key_weight, value_weight, queries, group_scale, new_kv, found)
+
+
+def finish_kernel(keys, values, smooth, att, cache_ref, smooth_ref, att_ref):
+    cache_ref[:, 0, :] = keys[...]
+    cache_ref[:, 1, :] = values[...]
+    smooth_ref[...] = smooth[...]
+    att_ref[...] = att[...]
+
+
+def finish(keys, values, smooth, att):
+    tokens, columns = keys.shape
+    tiles = 4
+    rows, wide = tokens // tiles, att.shape[1] // tiles
+    return pl.pallas_call(
+        finish_kernel,
+        grid=(tiles,),
+        out_shape=(
+            jax.ShapeDtypeStruct((tokens, 2, columns), keys.dtype),
+            jax.ShapeDtypeStruct(smooth.shape, smooth.dtype),
+            jax.ShapeDtypeStruct(att.shape, att.dtype),
+        ),
+        in_specs=[
+            pl.BlockSpec((rows, columns), lambda i: (i, 0)),
+            pl.BlockSpec((rows, columns), lambda i: (i, 0)),
+            pl.BlockSpec(smooth.shape, lambda i: (0, 0)),
+            pl.BlockSpec((att.shape[0], wide), lambda i: (0, i)),
+        ],
+        out_specs=(
+            pl.BlockSpec((rows, 2, columns), lambda i: (i, 0, 0)),
+            pl.BlockSpec(smooth.shape, lambda i: (0, 0)),
+            pl.BlockSpec((att.shape[0], wide), lambda i: (0, i)),
+        ),
+        name="finish",
+    )(keys, values, smooth, att)
 
 
 def on_device(
@@ -646,7 +758,7 @@
         new_kv.reshape(steps * requests, 2 * columns),
         found,
     )
-    kv_cache = jnp.stack([keys, values], axis=1)
+    kv_cache, smoothing, attention = finish(keys, values, smoothing, attention)
     return (
         kv_cache,
         smoothing.reshape(columns),

time: 127 us -> 101 us (0.80)
  Pallas kernels: 119 us -> 99.1 us
  local copies, waits for them, and re-layouts: 6.21 us -> 1.38 us
  other arithmetic: 1.3 us -> 0 us
    pallas_call x1, Pallas kernels: 117 us -> 93 us  [decode(): pl.pallas_call(decode_kernel, out_shape=(jax.ShapeDtypeStruct((tokens, co...]
    unnamed x4 -> x1, local copies, waits for them, and re-layouts: 6.21 us -> 1.38 us
    pallas_call x0 -> x1, Pallas kernels: none -> 4.34 us  [finish(): pl.pallas_call(finish_kernel, grid=(tiles,), out_shape=(jax.ShapeDtypeStr...]
    another operation x1 -> x0, other arithmetic: 1.3 us -> none  [on_device(): kv_cache = jnp.stack([keys, values], axis=1)]
where the time goes in v3:
time: 101 us
  Pallas kernels  99.1 us (98%)
  local copies, waits for them, and re-layouts  1.38 us (1%)
    pallas_call x1, Pallas kernels, decode(): pl.pallas_call(decode_kernel, out_shape=(jax.ShapeDtypeStruct((tokens, co...  93 us
    pallas_call x1, Pallas kernels, finish(): pl.pallas_call(finish_kernel, grid=(tiles,), out_shape=(jax.ShapeDtypeStr...  4.34 us

profile of v3, /device:TPU:1, one launch (start us, length us, event | category | flops | bytes accessed | tf_op | source)
XLA Modules:
  0.0 101.1 jit_solution(11339964468110758144)
XLA Ops:
  0.6 1.8 %find_pages.1.found_ref = s32[24,256]{1,0:T(8,128)} custom-call(s32[32,256]{1,0:T(8,128)} %bitcast.10, s32[1,256]{1,0:T(1,128)} %bitcast.11), custom_call_target="tpu_custom_call" | custom-call | tf_op jit(solution)/shard_map/find_pages/pallas_call | solution.py:235
  2.4 1.4 %copy.11 = bf16[4,8,2,256]{3,1,2,0:T(8,128)(2,1)} copy(bf16[4,8,2,256]{3,2,1,0:T(2,128)(2,1)} %param.12) | data formatting | bytes 65536
  3.8 93.0 %decode.1 = (bf16[1024,256]{1,0:T(8,128)(2,1)}, bf16[1024,256]{1,0:T(8,128)(2,1)}, f32[1,256]{1,0:T(1,128)}, bf16[32,2048]{1,0:T(8,128)(2,1)}) custom-call(bf16[1024,8192]{1,0:T(8,128)(2,1)} %hidden_hbm.1, bf16[128,256]{1,0:T(8,128)(2,1)} %wk_hbm.1, bf16[128,256]{1,0:T(8,128)(2,1)} %wv_hbm.1, bf16[32,2048]{1,0:T(8,128)(2,1)} %bitcast.8, f32[2,256]{1,0:T(2,128)} %scale_ref.1, ...), custom_call_target="tpu_custom_call" | custom-call | tf_op jit(solution)/shard_map/decode/pallas_call | solution.py:665
  96.8 4.3 %finish.1 = (bf16[1024,2,256]{2,1,0:T(2,128)(2,1)}, f32[1,256]{1,0:T(1,128)}, bf16[32,2048]{1,0:T(8,128)(2,1)}) custom-call(bf16[1024,256]{1,0:T(8,128)(2,1)} %get-tuple-element.10.keys, bf16[1024,256]{1,0:T(8,128)(2,1)} %get-tuple-element.11.values, f32[1,256]{1,0:T(1,128)} %get-tuple-element.12.smooth, bf16[32,2048]{1,0:T(8,128)(2,1)} %get-tuple-element.13.att), custom_call_target="tpu_custom_call" | custom-call | tf_op jit(solution)/shard_map/finish/pallas_call | solution.py:723

commit v4 on v3

--- a/solution.py
+++ b/solution.py
@@ -169,7 +169,7 @@
 
 
 STEPS_GATHER = 7
-QUERY_LAG = 3
+QUERY_LAG = 2
 def friends(torus):
     ring = [(torus.at(0, dz), torus.core) for dz in (1, -1, 2, -2, 3, -3, 4)]
     ring += [(torus.at(0, dz), 1 - torus.core) for dz in (0, 1, -1, 2, -2, 3, -3, 4)]
@@ -277,15 +277,17 @@
         self.got, self.got_stat = got, got_stat
         self.send_sem, self.recv_sem = send_sem, recv_sem
 
-    def copies(self, g, axis, way):
+    def copies(self, g, axis, way, slot=None, peer=None):
         step = 1 - 2 * way
-        peer = self.torus.at(step, 0) if axis == Y_AXIS else self.torus.at(0, step)
+        if peer is None:
+            peer = self.torus.at(step, 0) if axis == Y_AXIS else self.torus.at(0, step)
+        slot = g if slot is None else slot
         return [
             pltpu.make_async_remote_copy(
                 src_ref=src.at[g],
-                dst_ref=dst.at[axis, way, g],
+                dst_ref=dst.at[axis, way, slot],
                 send_sem=self.send_sem.at[k],
-                recv_sem=self.recv_sem.at[k, axis, way, g],
+                recv_sem=self.recv_sem.at[k, axis, way, slot],
                 device_id={"seq": peer},
                 device_id_type=pl.DeviceIdType.MESH,
             )
@@ -294,24 +296,36 @@
             )
         ]
 
+    def kept(self, at):
+        return self.stat[at, 0:1], self.stat[at, 1:2], self.part[at]
+
+    def keep(self, at, top, total, summed):
+        self.part[at] = summed
+        self.stat[at] = jnp.concatenate([top, total], axis=0)
+
     def gathered(self, g, arrivals, more=()):
-        parts = [(self.stat[g, 0:1], self.stat[g, 1:2], self.part[g]), *more]
-        for axis, way in arrivals:
-            for copy in self.copies(g, axis, way):
+        parts = [self.kept(g), *more]
+        for axis, way, *direct in arrivals:
+            slot = direct[0] if direct else g
+            for copy in self.copies(g, axis, way, slot):
                 copy.wait_recv()
-            stat = self.got_stat[axis, way, g]
-            parts.append((stat[0:1], stat[1:2], self.got[axis, way, g].astype(jnp.float32)))
+            stat = self.got_stat[axis, way, slot]
+            parts.append((stat[0:1], stat[1:2], self.got[axis, way, slot].astype(jnp.float32)))
         return fold(parts) if len(parts) > 1 else parts[0]
 
-    def send(self, dy, dz, arrivals, axis, way):
+    def send(self, dy, dz, arrivals, axis, way, slot=None, peer=None):
         g = self.torus.at(dy, dz)
         top, total, summed = self.gathered(g, arrivals)
         self.out[g] = summed.astype(jnp.bfloat16)
         self.out_stat[g] = jnp.concatenate([top, total], axis=0)
-        for copy in self.copies(g, axis, way):
+        for copy in self.copies(g, axis, way, slot, peer):
             copy.start()
 
-    def y_first(self, attend_to):
+    def finish(self, arrivals, fresh):
+        me = self.torus.at(0, 0)
+        self.keep(me, *self.gathered(me, arrivals, more=(self.kept(fresh),)))
+
+    def y_first(self, attend_to, chores):
         order = (4, -3, 3, -2, 2, -1, 1, 0)
         up, down = (Y_AXIS, 0), (Y_AXIS, 1)
 
@@ -335,13 +349,15 @@
             else:
                 self.send(1, dz, (up,), *up)
         row(0)
-        self.send(0, 4, (up, down), Z_AXIS, 0)
-        self.send(0, -3, (up, down), Z_AXIS, 1)
-        for dz in (3, -2, 2, -1, 1):
-            way = 0 if dz > 0 else 1
-            self.send(0, dz, (up, down, (Z_AXIS, way)), Z_AXIS, way)
-
-    def z_first(self, attend_to):
+        me = self.torus.at(0, 0)
+        for dz in order[:-1]:
+            self.send(0, dz, (up, down), Z_AXIS, 0, me, self.torus.at(0, dz))
+        for chore in chores:
+            chore()
+        straight = [(Z_AXIS, 0, self.torus.at(0, dz)) for dz in (1, -1, 2, -2, 3, -3, 4)]
+        self.finish((up, down, *straight), CHIPS)
+
+    def z_first(self, attend_to, chores):
         right, left = (Z_AXIS, 0), (Z_AXIS, 1)
         rows = (2, 1, -1, 0)
 
@@ -369,15 +385,21 @@
                 self.send(dy, dz, (right,), *right)
                 self.send(dy, -dz, (left,), *left)
         columns(0, NY)
+        chores[0]()
         self.send(2, 0, (right, left), Y_AXIS, 0)
         self.send(-1, 0, (right, left), Y_AXIS, 1)
+        for chore in chores[1:3]:
+            chore()
         self.send(1, 0, (right, left, (Y_AXIS, 0)), Y_AXIS, 0)
+        for chore in chores[3:]:
+            chore()
+        self.finish((right, left, (Y_AXIS, 0), (Y_AXIS, 1)), CHIPS)
 
 
 def decode_kernel(
     hidden_hbm, wk_hbm, wv_hbm, query_hbm, scale_ref, new_ref, found_ref,
-    keys_ref, values_ref, smooth_ref, att_ref,
-    hid, wk, wv, mz, my, qs, acc, kbuf, vbuf, kout, vout, part, stat, out, out_stat, got, got_stat,
+    cache_ref, smooth_ref, att_ref,
+    hid, wk, wv, mz, my, qs, acc, kraw, kbuf, vbuf, vout, fresh_kv, part, stat, out, out_stat, got, got_stat,
     att_out,
     local_sem, hid_sem, send_sem, recv_sem, swap_send, swap_recv, peak_sem, half_sem,
     part_send, part_recv,
@@ -462,20 +484,22 @@
     my_pages = pl.ds(pl.multiple_of(core * pages, pages), pages)
     their_pages = pl.ds(pl.multiple_of((1 - core) * pages, pages), pages)
 
-    def half(k, leaving, whole, at):
+    def to_partner(k, src, dst):
         return pltpu.make_async_remote_copy(
-            src_ref=leaving,
-            dst_ref=whole.at[at],
+            src_ref=src,
+            dst_ref=dst,
             send_sem=half_sem.at[k, 0],
             recv_sem=half_sem.at[k, 1],
             device_id={"rep": 1 - core},
             device_id_type=pl.DeviceIdType.MESH,
         )
 
-    def share(k, full, whole, leaving):
-        leaving[...] = full[:, theirs].reshape(leaving.shape)
-        whole[my_pages] = full[:, mine].reshape(leaving.shape)
-        half(k, leaving, whole, my_pages).start()
+    def clip(x, kind, lanes):
+        scale = scale_ref[kind : kind + 1, lanes]
+        return jnp.clip(x, -8.0 * scale, 7.0 * scale).astype(jnp.bfloat16)
+
+    keys_over = to_partner(0, acc.at[0, :, theirs], kraw)
+    values_over = to_partner(1, vout, vbuf.at[my_pages])
 
     ring, column = friends(torus)
     place = core * NZ + torus.z
@@ -505,19 +529,26 @@
             for copy in own_q:
                 copy.wait()
         for stream_i, start in ((s_k, 0), (s_v, 0), (s_qa, q_lag), (s_qb, q_lag)):
+            if i == 5 and stream_i is s_qa:
+                for copy in hid_copies:
+                    copy.wait()
+                multiply(s_k, wk, acc.at[0], 0)
             if 0 <= i - start < STEPS_GATHER:
                 stream_i.step(i - start)
+        if i == 0:
+            for kind in range(2):
+                fresh_kv[kind] = (
+                    new_ref[:, :, kind, :].astype(jnp.float32).reshape(steps_reqs, columns)
+                )
         if i == 5:
-            for copy in hid_copies:
-                copy.wait()
-            multiply(s_k, wk, acc.at[0], 0)
-            multiply(s_v, wv, acc.at[1], 0)
-        if i == 6:
             multiply(s_k, wk, acc.at[0], 1)
             multiply(s_k, wk, acc.at[0], -1)
+        if i == 6:
             multiply(s_k, wk, acc.at[0], 2)
             mz[place] = jnp.max(jnp.abs(acc[0]).reshape(tokens // 8, 8, columns), axis=0)
             tell(mz, place, 0, ring)
+            keys_over.start()
+            multiply(s_v, wv, acc.at[1], 0)
         if i == 7:
             multiply(s_v, wv, acc.at[1], 1)
             multiply(s_v, wv, acc.at[1], -1)
@@ -526,20 +557,12 @@
             my[torus.y] = jnp.max(mz[...], axis=0)
             tell(my, torus.y, 1, column)
             multiply(s_v, wv, acc.at[1], 2)
-        if i == 9:
-            values_ref[...] = jnp.clip(
-                acc[1], -8.0 * scale_ref[1:2, :], 7.0 * scale_ref[1:2, :]
-            ).astype(jnp.bfloat16)
-            share(0, values_ref, vbuf, vout)
+            vout[...] = clip(acc[1, :, theirs], 1, theirs).reshape(vout.shape)
+            values_over.start()
+            vbuf[my_pages] = clip(acc[1, :, mine], 1, mine).reshape(vout.shape)
     heard(my, 1, column).wait_recv()
     peak = jnp.max(my[...], axis=0)
-    smooth = jnp.sqrt(jnp.max(peak, axis=0, keepdims=True) + EPSILON)
-    smooth_ref[...] = smooth
-    keys_ref[...] = jnp.clip(
-        acc[0] / smooth, -8.0 * scale_ref[0:1, :], 7.0 * scale_ref[0:1, :]
-    ).astype(jnp.bfloat16)
-    share(1, keys_ref, kbuf, kout)
-
+    smooth_ref[...] = jnp.sqrt(jnp.max(peak, axis=0, keepdims=True) + EPSILON)
     my_smooth = smooth_ref[:, mine]
 
     def queries_of(g):
@@ -561,21 +584,10 @@
     key = lax.broadcasted_iota(jnp.int32, (PAGE, across), 0)
     request = lane % 8
 
-    fresh_keys = jnp.clip(
-        new_ref[:, mine].astype(jnp.float32) / my_smooth,
-        -8.0 * scale_ref[0:1, mine],
-        7.0 * scale_ref[0:1, mine],
-    ).astype(jnp.bfloat16)
-    fresh_values = jnp.clip(
-        new_ref[:, pl.ds(pl.multiple_of(columns + core * HD, HD), HD)].astype(jnp.float32),
-        -8.0 * scale_ref[1:2, mine],
-        7.0 * scale_ref[1:2, mine],
-    ).astype(jnp.bfloat16)
-    fresh_mask = (key % 8 == request) & (key // 8 <= (lane // 8) % (steps_reqs // 8))
-    fresh = attend(fresh_keys, fresh_values, queries_of(me), fresh_mask)
-
-    half(0, vout, vbuf, their_pages).wait_recv()
-    half(1, kout, kbuf, their_pages).wait_recv()
+    kbuf[my_pages] = clip(acc[0, :, mine] / my_smooth, 0, mine).reshape(vout.shape)
+    keys_over.wait_recv()
+    kbuf[their_pages] = clip(kraw[...] / my_smooth, 0, mine).reshape(vout.shape)
+    to_partner(1, vout, vbuf.at[their_pages]).wait_recv()
 
     def one_group(g):
         keys, values, masks = [], [], []
@@ -605,29 +617,48 @@
         torus, part, stat, out, out_stat, got, got_stat, part_send, part_recv
     )
 
+    def write_cache(quarter):
+        def chore():
+            at = pl.ds(quarter * (tokens // 4), tokens // 4)
+            every = slice(None)
+            cache_ref[at] = jnp.stack(
+                [
+                    clip(acc[0, at, :] / smooth_ref[...], 0, every),
+                    clip(acc[1, at, :], 1, every),
+                ],
+                axis=1,
+            )
+
+        return chore
+
+    def attend_fresh():
+        mask = (key % 8 == request) & (key // 8 <= (lane // 8) % (steps_reqs // 8))
+        partials.keep(
+            CHIPS,
+            *attend(
+                clip(fresh_kv[0, :, mine] / my_smooth, 0, mine),
+                clip(fresh_kv[1, :, mine], 1, mine),
+                queries_of(me),
+                mask,
+            ),
+        )
+
+    chores = [*(write_cache(quarter) for quarter in range(4)), attend_fresh]
+
     @pl.when(core == 0)
     def _():
-        partials.y_first(attend_to)
+        partials.y_first(attend_to, chores)
 
     @pl.when(core == 1)
     def _():
-        partials.z_first(attend_to)
-
-    top, total, summed = partials.gathered(
-        me, ((Y_AXIS, 0), (Y_AXIS, 1), (Z_AXIS, 0), (Z_AXIS, 1)), more=(fresh,)
-    )
+        partials.z_first(attend_to, chores)
+
+    top, total, summed = partials.kept(me)
     done = (summed / total).T.astype(jnp.bfloat16)
     for h in range(heads):
         att_out[:, h * HD : (h + 1) * HD] = done[h * steps_reqs : (h + 1) * steps_reqs]
     own_att = pl.ds(pl.multiple_of(core * half_q, half_q), half_q)
-    last = pltpu.make_async_remote_copy(
-        src_ref=att_out,
-        dst_ref=att_ref.at[:, own_att],
-        send_sem=half_sem.at[2, 0],
-        recv_sem=half_sem.at[2, 1],
-        device_id={"rep": 1 - core},
-        device_id_type=pl.DeviceIdType.MESH,
-    )
+    last = to_partner(2, att_out, att_ref.at[:, own_att])
     last.start()
     att_ref[:, own_att] = att_out[...]
 
@@ -638,8 +669,8 @@
     s_qb.sent_copy(qs.at[pl.ds(0, CHIPS - 1), 1]).wait_send()
     heard(mz, 0, ring).wait_send()
     heard(my, 1, column).wait_send()
-    half(0, vout, vbuf, my_pages).wait_send()
-    half(1, kout, kbuf, my_pages).wait_send()
+    keys_over.wait_send()
+    values_over.wait_send()
     for k, refs in enumerate((out, out_stat)):
         pltpu.make_async_remote_copy(
             src_ref=refs.at[pl.ds(0, CHIPS - 1)],
@@ -665,13 +696,12 @@
     return pl.pallas_call(
         decode_kernel,
         out_shape=(
-            jax.ShapeDtypeStruct((tokens, columns), bf16),
-            jax.ShapeDtypeStruct((tokens, columns), bf16),
+            jax.ShapeDtypeStruct((tokens, 2, columns), bf16),
             jax.ShapeDtypeStruct((1, columns), f32),
             jax.ShapeDtypeStruct((step_reqs, q_columns), bf16),
         ),
         in_specs=[any_spec, any_spec, any_spec, any_spec, vmem, vmem, smem],
-        out_specs=(vmem, vmem, vmem, vmem),
+        out_specs=(vmem, vmem, vmem),
         scratch_shapes=[
             pltpu.VMEM((tokens, depth), bf16),
             pltpu.VMEM((CHIPS, 2, rows, columns), bf16),
@@ -680,12 +710,13 @@
             pltpu.VMEM((NY, 8, columns), f32),
             pltpu.VMEM((CHIPS, 2, step_reqs // 2, q_columns // 2), bf16),
             pltpu.VMEM((2, tokens, columns), f32),
+            pltpu.VMEM((tokens, HD), f32),
             pltpu.VMEM((2 * pages, PAGE, HD), bf16),
             pltpu.VMEM((2 * pages, PAGE, HD), bf16),
             pltpu.VMEM((pages, PAGE, HD), bf16),
-            pltpu.VMEM((pages, PAGE, HD), bf16),
-            pltpu.VMEM((CHIPS, HD, across), f32),
-            pltpu.VMEM((CHIPS, 2, across), f32),
+            pltpu.VMEM((2, step_reqs, columns), f32),
+            pltpu.VMEM((CHIPS + 1, HD, across), f32),
+            pltpu.VMEM((CHIPS + 1, 2, across), f32),
             pltpu.VMEM((CHIPS, HD, across), bf16),
             pltpu.VMEM((CHIPS, 2, across), f32),
             pltpu.VMEM((2, 2, CHIPS, HD, across), bf16),
@@ -709,38 +740,46 @@
     )(hidden, key_weight, value_weight, queries, group_scale, new_kv, found)
 
 
-def finish_kernel(keys, values, smooth, att, cache_ref, smooth_ref, att_ref):
-    cache_ref[:, 0, :] = keys[...]
-    cache_ref[:, 1, :] = values[...]
-    smooth_ref[...] = smooth[...]
-    att_ref[...] = att[...]
-
-
-def finish(keys, values, smooth, att):
-    tokens, columns = keys.shape
-    tiles = 4
-    rows, wide = tokens // tiles, att.shape[1] // tiles
+def finish_kernel(*refs):
+    outputs = len(refs) // 3
+    sem = refs[-1]
+    pieces = []
+    for src, dst, via in zip(refs[:outputs], refs[outputs:], refs[2 * outputs :]):
+        count = 4 if len(src.shape) == 3 else 1
+        rows = src.shape[0] // count
+        pieces += [
+            tuple(r.at[pl.ds(k * rows, rows)] for r in (src, via, dst)) for k in range(count)
+        ]
+    legs = []
+    for k, (src, via, dst) in enumerate(pieces):
+        legs.append(
+            (
+                pltpu.make_async_copy(src, via, sem.at[k, 0]),
+                pltpu.make_async_copy(via, dst, sem.at[k, 1]),
+            )
+        )
+    for first, _ in legs:
+        first.start()
+    for first, second in legs:
+        first.wait()
+        second.start()
+    for _, second in legs:
+        second.wait()
+
+
+def finish(*arrays):
+    any_spec = pl.BlockSpec(memory_space=pl.ANY)
     return pl.pallas_call(
         finish_kernel,
-        grid=(tiles,),
-        out_shape=(
-            jax.ShapeDtypeStruct((tokens, 2, columns), keys.dtype),
-            jax.ShapeDtypeStruct(smooth.shape, smooth.dtype),
-            jax.ShapeDtypeStruct(att.shape, att.dtype),
-        ),
-        in_specs=[
-            pl.BlockSpec((rows, columns), lambda i: (i, 0)),
-            pl.BlockSpec((rows, columns), lambda i: (i, 0)),
-            pl.BlockSpec(smooth.shape, lambda i: (0, 0)),
-            pl.BlockSpec((att.shape[0], wide), lambda i: (0, i)),
+        out_shape=tuple(jax.ShapeDtypeStruct(a.shape, a.dtype) for a in arrays),
+        in_specs=[any_spec] * len(arrays),
+        out_specs=(any_spec,) * len(arrays),
+        scratch_shapes=[
+            *(pltpu.VMEM(a.shape, a.dtype) for a in arrays),
+            pltpu.SemaphoreType.DMA((6, 2)),
         ],
-        out_specs=(
-            pl.BlockSpec((rows, 2, columns), lambda i: (i, 0, 0)),
-            pl.BlockSpec(smooth.shape, lambda i: (0, 0)),
-            pl.BlockSpec((att.shape[0], wide), lambda i: (0, i)),
-        ),
         name="finish",
-    )(keys, values, smooth, att)
+    )(*arrays)
 
 
 def on_device(
@@ -748,17 +787,17 @@
 ):
     steps, requests, q_columns = decode_query.shape
     columns = key_weight.shape[1]
-    found = find_pages(page_table, lengths)
-    keys, values, smoothing, attention = decode(
-        hidden,
-        key_weight,
-        value_weight,
-        decode_query.reshape(steps * requests, q_columns),
-        group_scale,
-        new_kv.reshape(steps * requests, 2 * columns),
-        found,
-    )
-    kv_cache, smoothing, attention = finish(keys, values, smoothing, attention)
+    kv_cache, smoothing, attention = finish(
+        *decode(
+            hidden,
+            key_weight,
+            value_weight,
+            decode_query.reshape(steps * requests, q_columns),
+            group_scale,
+            new_kv,
+            find_pages(page_table, lengths),
+        )
+    )
     return (
         kv_cache,
         smoothing.reshape(columns),

time: 101 us -> 95 us (0.941)
  Pallas kernels: 99.1 us -> 93.9 us
  local copies, waits for them, and re-layouts: 1.38 us -> 0 us
    pallas_call x2, Pallas kernels: 97.3 us -> 92.1 us  [the longest x1 90 us: decode(): pl.pallas_call(decode_kernel, out_shape=(jax.ShapeDtypeStruct((tokens, 2,...]
    unnamed x1 -> x0, local copies, waits for them, and re-layouts: 1.38 us -> none
where the time goes in v4:
time: 95 us; the launch traced here: 94.7 us
  Pallas kernels  93.9 us (99%)
    pallas_call x1, Pallas kernels, decode(): pl.pallas_call(decode_kernel, out_shape=(jax.ShapeDtypeStruct((tokens, 2,...  90 us
    pallas_call x1, Pallas kernels, finish(): pl.pallas_call(finish_kernel, out_shape=tuple((jax.ShapeDtypeStruct(a.sha...  2.06 us

profile of v4, /device:TPU:1, one launch (start us, length us, event | category | flops | bytes accessed | tf_op | source)
XLA Modules:
  0.0 94.7 jit_solution(13371992949734221036)
XLA Ops:
  0.6 1.8 %find_pages.1.found_ref = s32[24,256]{1,0:T(8,128)} custom-call(s32[32,256]{1,0:T(8,128)} %bitcast.6, s32[1,256]{1,0:T(1,128)} %bitcast.7), custom_call_target="tpu_custom_call" | custom-call | tf_op jit(solution)/shard_map/find_pages/pallas_call | solution.py:235
  2.4 90.0 %decode.1 = (bf16[1024,2,256]{2,1,0:T(2,128)(2,1)}, f32[1,256]{1,0:T(1,128)}, bf16[32,2048]{1,0:T(8,128)(2,1)}) custom-call(bf16[1024,8192]{1,0:T(8,128)(2,1)} %hidden_hbm.1, bf16[128,256]{1,0:T(8,128)(2,1)} %wk_hbm.1, bf16[128,256]{1,0:T(8,128)(2,1)} %wv_hbm.1, bf16[32,2048]{1,0:T(8,128)(2,1)} %bitcast.5, f32[2,256]{1,0:T(2,128)} %scale_ref.1, ...), custom_call_target="tpu_custom_call" | custom-call | tf_op jit(solution)/shard_map/decode/pallas_call | solution.py:696
  92.4 2.1 %finish.1 = (bf16[1024,2,256]{2,1,0:T(2,128)(2,1)}, f32[1,256]{1,0:T(1,128)}, bf16[32,2048]{1,0:T(8,128)(2,1)}) custom-call(bf16[1024,2,256]{2,1,0:T(2,128)(2,1)} %get-tuple-element.9.refs_0_, f32[1,256]{1,0:T(1,128)} %get-tuple-element.10.refs_1_, bf16[32,2048]{1,0:T(8,128)(2,1)} %get-tuple-element.11.refs_2_), custom_call_target="tpu_custom_call" | custom-call | tf_op jit(solution)/shard_map/finish/pallas_call | solution.py:772

commit v5 on v4

--- a/solution.py
+++ b/solution.py
@@ -18,6 +18,7 @@
 
 EPSILON = 1e-05
 NEGATIVE = -1e30
+EMPTY = -1e29
 
 
 class Torus:
@@ -254,12 +255,16 @@
     )
 
 
-def attend(keys, values, queries, mask):
-    scores = jnp.where(mask, below(keys, queries) * HD ** (-0.5), NEGATIVE)
-    top = jnp.max(scores, axis=0, keepdims=True)
-    weights = jnp.where(mask, jnp.exp(scores - top), 0.0)
-    total = jnp.sum(weights, axis=0, keepdims=True)
-    return top, total, weighed(values, weights.astype(jnp.bfloat16))
+def attend(jobs):
+    scores = [
+        jnp.where(mask, below(keys, queries) * HD ** (-0.5), NEGATIVE)
+        for keys, _, queries, mask in jobs
+    ]
+    tops = [jnp.maximum(jnp.max(x, axis=0, keepdims=True), EMPTY) for x in scores]
+    weights = [jnp.exp(x - top) for x, top in zip(scores, tops)]
+    totals = [jnp.sum(x, axis=0, keepdims=True) for x in weights]
+    sums = [weighed(job[1], x.astype(jnp.bfloat16)) for job, x in zip(jobs, weights)]
+    return list(zip(tops, totals, sums))
 
 
 def fold(parts):
@@ -325,75 +330,91 @@
         me = self.torus.at(0, 0)
         self.keep(me, *self.gathered(me, arrivals, more=(self.kept(fresh),)))
 
-    def y_first(self, attend_to, chores):
-        order = (4, -3, 3, -2, 2, -1, 1, 0)
+    def y_first(self, attend_at, chores):
         up, down = (Y_AXIS, 0), (Y_AXIS, 1)
 
-        def row(dy):
-            attend_to(NZ, lambda k: self.torus.at(dy, 4 - k))
-
-        row(2)
-        for dz in order:
-            self.send(2, dz, (), Y_AXIS, dz % 2)
-        row(1)
-        for dz in order:
-            if dz % 2:
-                self.send(1, dz, (), *up)
-        row(-1)
-        for dz in order:
-            if dz % 2 == 0:
-                self.send(-1, dz, (), *down)
-        for dz in order:
-            if dz % 2:
-                self.send(-1, dz, (down,), *down)
-            else:
-                self.send(1, dz, (up,), *up)
-        row(0)
+        def far(k):
+            dz = 4 - 2 * k
+            attend_at((2, dz), (2, dz - 1))
+            self.send(2, dz, (), *up)
+            self.send(2, dz - 1, (), *down)
+
+        def near(k):
+            dz = 4 - 2 * k
+            attend_at((1, dz - 1), (-1, dz))
+            self.send(1, dz - 1, (), *up)
+            self.send(-1, dz, (), *down)
+
+        def near_passing(k):
+            dz = 4 - 2 * k
+            attend_at((1, dz), (-1, dz - 1))
+            self.send(1, dz, (up,), *up)
+            self.send(-1, dz - 1, (down,), *down)
+
+        for body in (far, near, near_passing):
+            repeat(NZ // 2, body)
+        repeat(NZ // 2, lambda k: attend_at((0, 4 - 2 * k), (0, 3 - 2 * k)))
         me = self.torus.at(0, 0)
-        for dz in order[:-1]:
+        for dz in (4, -3, 3, -2, 2, -1, 1):
             self.send(0, dz, (up, down), Z_AXIS, 0, me, self.torus.at(0, dz))
         for chore in chores:
             chore()
         straight = [(Z_AXIS, 0, self.torus.at(0, dz)) for dz in (1, -1, 2, -2, 3, -3, 4)]
         self.finish((up, down, *straight), CHIPS)
 
-    def z_first(self, attend_to, chores):
+    def z_first(self, attend_at, chores):
         right, left = (Z_AXIS, 0), (Z_AXIS, 1)
-        rows = (2, 1, -1, 0)
-
-        def columns(dz, count):
-            attend_to(
-                count,
-                lambda k: self.torus.at(
-                    2 - lax.rem(k, NY), dz * (1 - 2 * lax.div(k, NY)) if dz else 0
-                ),
-            )
-
-        columns(4, NY)
-        for dy in rows:
-            self.send(dy, 4, (), Z_AXIS, dy % 2)
-        columns(3, 2 * NY)
-        for dy in rows:
-            way = 1 - dy % 2
-            self.send(dy, -3 if way else 3, (), Z_AXIS, way)
-        for dy in rows:
-            way = dy % 2
-            self.send(dy, -3 if way else 3, ((Z_AXIS, way),), Z_AXIS, way)
-        for dz in (2, 1):
-            columns(dz, 2 * NY)
-            for dy in rows:
+
+        def far(k):
+            dy = 2 - 2 * k
+            attend_at((dy, 4), (dy - 1, 4))
+            self.send(dy, 4, (), *right)
+            self.send(dy - 1, 4, (), *left)
+
+        def near(k):
+            dy = 2 - 2 * k
+            attend_at((dy, -3), (dy - 1, 3))
+            self.send(dy, -3, (), *left)
+            self.send(dy - 1, 3, (), *right)
+
+        def near_passing(k):
+            dy = 2 - 2 * k
+            attend_at((dy, 3), (dy - 1, -3))
+            self.send(dy, 3, (right,), *right)
+            self.send(dy - 1, -3, (left,), *left)
+
+        for body in (far, near, near_passing):
+            repeat(NY // 2, body)
+
+        def both(dz):
+            def body(k):
+                dy = 2 - k
+                attend_at((dy, dz), (dy, -dz))
                 self.send(dy, dz, (right,), *right)
                 self.send(dy, -dz, (left,), *left)
-        columns(0, NY)
-        chores[0]()
-        self.send(2, 0, (right, left), Y_AXIS, 0)
-        self.send(-1, 0, (right, left), Y_AXIS, 1)
-        for chore in chores[1:3]:
+
+            return body
+
+        for dz in (2, 1):
+            repeat(NY, both(dz))
+        repeat(NY // 2, lambda k: attend_at((2 - 2 * k, 0), (1 - 2 * k, 0)))
+        for chore in chores[:2]:
             chore()
-        self.send(1, 0, (right, left, (Y_AXIS, 0)), Y_AXIS, 0)
-        for chore in chores[3:]:
+        me = self.torus.at(0, 0)
+        for dy in (2, 1, -1):
+            self.send(dy, 0, (right, left), Y_AXIS, 0, me, self.torus.at(dy, 0))
+        for chore in chores[2:]:
             chore()
-        self.finish((right, left, (Y_AXIS, 0), (Y_AXIS, 1)), CHIPS)
+        straight = [(Y_AXIS, 0, self.torus.at(dy, 0)) for dy in (1, -1, 2)]
+        self.finish((right, left, *straight), CHIPS)
+
+
+def repeat(count, body):
+    def step(k, carry):
+        body(k)
+        return carry
+
+    lax.fori_loop(0, count, step, 0)
 
 
 def decode_kernel(
@@ -589,29 +610,24 @@
     kbuf[their_pages] = clip(kraw[...] / my_smooth, 0, mine).reshape(vout.shape)
     to_partner(1, vout, vbuf.at[their_pages]).wait_recv()
 
-    def one_group(g):
+    def job_of(g):
         keys, values, masks = [], [], []
         for e in range(SLOTS):
             who, page, count = (found_ref[SLOTS * f + e, g * 8] for f in range(3))
             keys.append(kbuf[page])
             values.append(vbuf[page])
             masks.append((request == who) & (key < count))
-        top, total, summed = attend(
+        return (
             jnp.concatenate(keys, axis=0),
             jnp.concatenate(values, axis=0),
             queries_of(g),
             jnp.concatenate(masks, axis=0),
         )
-        part[g] = summed
-        stat[g] = jnp.concatenate([top, total], axis=0)
-
-    def attend_to(count, group):
-        def two(i, carry):
-            one_group(group(2 * i))
-            one_group(group(2 * i + 1))
-            return carry
-
-        lax.fori_loop(0, count // 2, two, 0)
+
+    def attend_at(*places):
+        groups = [torus.at(dy, dz) for dy, dz in places]
+        for g, found in zip(groups, attend([job_of(g) for g in groups])):
+            partials.keep(g, *found)
 
     partials = Partials(
         torus, part, stat, out, out_stat, got, got_stat, part_send, part_recv
@@ -633,25 +649,23 @@
 
     def attend_fresh():
         mask = (key % 8 == request) & (key // 8 <= (lane // 8) % (steps_reqs // 8))
-        partials.keep(
-            CHIPS,
-            *attend(
-                clip(fresh_kv[0, :, mine] / my_smooth, 0, mine),
-                clip(fresh_kv[1, :, mine], 1, mine),
-                queries_of(me),
-                mask,
-            ),
-        )
+        job = (
+            clip(fresh_kv[0, :, mine] / my_smooth, 0, mine),
+            clip(fresh_kv[1, :, mine], 1, mine),
+            queries_of(me),
+            mask,
+        )
+        partials.keep(CHIPS, *attend([job])[0])
 
     chores = [*(write_cache(quarter) for quarter in range(4)), attend_fresh]
 
     @pl.when(core == 0)
     def _():
-        partials.y_first(attend_to, chores)
+        partials.y_first(attend_at, chores)
 
     @pl.when(core == 1)
     def _():
-        partials.z_first(attend_to, chores)
+        partials.z_first(attend_at, chores)
 
     top, total, summed = partials.kept(me)
     done = (summed / total).T.astype(jnp.bfloat16)

time: 95 us -> 91 us (0.958)
  Pallas kernels: 93.9 us -> 89.7 us
    pallas_call x1, Pallas kernels: 90 us -> 85.9 us  [decode(): pl.pallas_call(decode_kernel, out_shape=(jax.ShapeDtypeStruct((tokens, 2,...]
where the time goes in v5:
time: 91 us; the launch traced here: 90.5 us
  Pallas kernels  89.7 us (99%)
    pallas_call x1, Pallas kernels, decode(): pl.pallas_call(decode_kernel, out_shape=(jax.ShapeDtypeStruct((tokens, 2,...  85.9 us
    pallas_call x1, Pallas kernels, finish(): pl.pallas_call(finish_kernel, out_shape=tuple((jax.ShapeDtypeStruct(a.sha...  2.06 us

profile of v5, /device:TPU:1, one launch (start us, length us, event | category | flops | bytes accessed | tf_op | source)
XLA Modules:
  0.0 90.5 jit_solution(10012161505321349560)
XLA Ops:
  0.6 1.8 %find_pages.1.found_ref = s32[24,256]{1,0:T(8,128)} custom-call(s32[32,256]{1,0:T(8,128)} %bitcast.6, s32[1,256]{1,0:T(1,128)} %bitcast.7), custom_call_target="tpu_custom_call" | custom-call | tf_op jit(solution)/shard_map/find_pages/pallas_call | solution.py:236
  2.4 85.9 %decode.1 = (bf16[1024,2,256]{2,1,0:T(2,128)(2,1)}, f32[1,256]{1,0:T(1,128)}, bf16[32,2048]{1,0:T(8,128)(2,1)}) custom-call(bf16[1024,8192]{1,0:T(8,128)(2,1)} %hidden_hbm.1, bf16[128,256]{1,0:T(8,128)(2,1)} %wk_hbm.1, bf16[128,256]{1,0:T(8,128)(2,1)} %wv_hbm.1, bf16[32,2048]{1,0:T(8,128)(2,1)} %bitcast.5, f32[2,256]{1,0:T(2,128)} %scale_ref.1, ...), custom_call_target="tpu_custom_call" | custom-call | tf_op jit(solution)/shard_map/decode/pallas_call | solution.py:710
  88.3 2.1 %finish.1 = (bf16[1024,2,256]{2,1,0:T(2,128)(2,1)}, f32[1,256]{1,0:T(1,128)}, bf16[32,2048]{1,0:T(8,128)(2,1)}) custom-call(bf16[1024,2,256]{2,1,0:T(2,128)(2,1)} %get-tuple-element.9.refs_0_, f32[1,256]{1,0:T(1,128)} %get-tuple-element.10.refs_1_, bf16[32,2048]{1,0:T(8,128)(2,1)} %get-tuple-element.11.refs_2_), custom_call_target="tpu_custom_call" | custom-call | tf_op jit(solution)/shard_map/finish/pallas_call | solution.py:786

commit v6 on v5

--- a/solution.py
+++ b/solution.py
@@ -170,7 +170,7 @@
 
 
 STEPS_GATHER = 7
-QUERY_LAG = 2
+QUERY_LAG = 3
 def friends(torus):
     ring = [(torus.at(0, dz), torus.core) for dz in (1, -1, 2, -2, 3, -3, 4)]
     ring += [(torus.at(0, dz), 1 - torus.core) for dz in (0, 1, -1, 2, -2, 3, -3, 4)]
@@ -193,51 +193,39 @@
 SLOTS = 8
 
 
-def find_kernel(table_ref, length_ref, found_ref):
-    chip = lax.axis_index("seq")
-    table = table_ref[...]
+def find_pages(table, lengths):
     slots, requests = table.shape
     slot = lax.broadcasted_iota(jnp.int32, table.shape, 0)
     lane = lax.broadcasted_iota(jnp.int32, table.shape, 1)
-    left = length_ref[...] - slot * PAGE
-    mine = ((left > 0) & (table // (2 * PAGE) == chip)).astype(jnp.float32)
-    row = lax.broadcasted_iota(jnp.int32, (slots, slots), 0)
-    column = lax.broadcasted_iota(jnp.int32, (slots, slots), 1)
-    above = jnp.dot(
-        (column < row).astype(jnp.float32), mine, preferred_element_type=jnp.float32
-    )
+    chip = lax.axis_index("seq")
+    left = lengths - slot * PAGE
+    mine = jnp.where((left > 0) & (table // (2 * PAGE) == chip), 1, 0)
+    upto = mine
+    for k in (1, 2, 4, 8, 16):
+        upto = upto + jnp.where(slot >= k, pltpu.roll(upto, k, 0), 0)
     whole = jnp.broadcast_to(jnp.sum(mine, axis=0, keepdims=True), (8, requests))
-    a = lax.broadcasted_iota(jnp.int32, (requests, requests), 0)
-    b = lax.broadcasted_iota(jnp.int32, (requests, requests), 1)
-    same = a // 8 == b // 8
-    before = jnp.dot(
-        whole, (same & (a < b)).astype(jnp.float32), preferred_element_type=jnp.float32
-    )
-    rank = jnp.where(mine > 0.0, above + before[0:1], -1.0)
-    fields = (
-        (lane % 8).astype(jnp.float32),
-        (table % (2 * PAGE)).astype(jnp.float32),
-        jnp.minimum(left, PAGE).astype(jnp.float32),
-    )
+    across = lax.broadcasted_iota(jnp.int32, whole.shape, 1) % 8
+    before = whole
+    for k in (1, 2, 4):
+        before = before + jnp.where(across >= k, pltpu.roll(before, k, 1), 0)
+    before = before - whole
+    rank = jnp.where(mine > 0, upto - 1 + before[0:1], -1)
+    fields = (lane % 8, table % (2 * PAGE), jnp.minimum(left, PAGE))
     picked = jnp.concatenate(
         [
-            jnp.sum(jnp.where(rank == e, field, 0.0), axis=0, keepdims=True)
+            jnp.sum(jnp.where(rank == e, field, 0), axis=0, keepdims=True)
             for field in fields
             for e in range(SLOTS)
         ],
         axis=0,
     )
-    spread = jnp.dot(picked, same.astype(jnp.float32), preferred_element_type=jnp.float32)
-    found_ref[...] = spread.astype(jnp.int32)
-
-
-def find_pages(page_table, lengths):
-    requests, slots = page_table.shape
-    return pl.pallas_call(
-        find_kernel,
-        out_shape=jax.ShapeDtypeStruct((3 * SLOTS, requests), jnp.int32),
-        name="find_pages",
-    )(page_table.T, lengths.reshape(1, requests))
+    side = lax.broadcasted_iota(jnp.int32, picked.shape, 1)
+    for k in (1, 2, 4):
+        other = jnp.where(
+            side // k % 2 == 1, pltpu.roll(picked, k, 1), pltpu.roll(picked, requests - k, 1)
+        )
+        picked = picked + other
+    return picked
 
 
 Y_AXIS, Z_AXIS = 0, 1
@@ -334,29 +322,31 @@
         up, down = (Y_AXIS, 0), (Y_AXIS, 1)
 
         def far(k):
-            dz = 4 - 2 * k
+            dz = lax.rem(4 + 2 * k, NZ)
             attend_at((2, dz), (2, dz - 1))
             self.send(2, dz, (), *up)
             self.send(2, dz - 1, (), *down)
 
         def near(k):
-            dz = 4 - 2 * k
+            dz = lax.rem(4 + 2 * k, NZ)
             attend_at((1, dz - 1), (-1, dz))
             self.send(1, dz - 1, (), *up)
             self.send(-1, dz, (), *down)
 
         def near_passing(k):
-            dz = 4 - 2 * k
+            dz = lax.rem(4 + 2 * k, NZ)
             attend_at((1, dz), (-1, dz - 1))
             self.send(1, dz, (up,), *up)
             self.send(-1, dz - 1, (down,), *down)
 
         for body in (far, near, near_passing):
             repeat(NZ // 2, body)
-        repeat(NZ // 2, lambda k: attend_at((0, 4 - 2 * k), (0, 3 - 2 * k)))
         me = self.torus.at(0, 0)
-        for dz in (4, -3, 3, -2, 2, -1, 1):
-            self.send(0, dz, (up, down), Z_AXIS, 0, me, self.torus.at(0, dz))
+        for pair in ((4, 3), (-2, -3), (0, -1), (2, 1)):
+            attend_at(*((0, dz) for dz in pair))
+            for dz in pair:
+                if dz:
+                    self.send(0, dz, (up, down), Z_AXIS, 0, me, self.torus.at(0, dz))
         for chore in chores:
             chore()
         straight = [(Z_AXIS, 0, self.torus.at(0, dz)) for dz in (1, -1, 2, -2, 3, -3, 4)]
@@ -418,9 +408,9 @@
 
 
 def decode_kernel(
-    hidden_hbm, wk_hbm, wv_hbm, query_hbm, scale_ref, new_ref, found_ref,
+    hidden_hbm, wk_hbm, wv_hbm, query_hbm, scale_ref, new_ref, table_ref, length_ref,
     cache_ref, smooth_ref, att_ref,
-    hid, wk, wv, mz, my, qs, acc, kraw, kbuf, vbuf, vout, fresh_kv, part, stat, out, out_stat, got, got_stat,
+    hid, wk, wv, mz, my, qs, acc, kraw, kbuf, vbuf, vout, fresh_kv, found_v, found_ref, part, stat, out, out_stat, got, got_stat,
     att_out,
     local_sem, hid_sem, send_sem, recv_sem, swap_send, swap_recv, peak_sem, half_sem,
     part_send, part_recv,
@@ -521,6 +511,7 @@
 
     keys_over = to_partner(0, acc.at[0, :, theirs], kraw)
     values_over = to_partner(1, vout, vbuf.at[my_pages])
+    found_copy = pltpu.make_async_copy(found_v, found_ref, local_sem.at[4])
 
     ring, column = friends(torus)
     place = core * NZ + torus.z
@@ -549,7 +540,7 @@
         if i == q_lag:
             for copy in own_q:
                 copy.wait()
-        for stream_i, start in ((s_k, 0), (s_v, 0), (s_qa, q_lag), (s_qb, q_lag)):
+        for stream_i, start in ((s_k, 0), (s_v, 1), (s_qa, q_lag), (s_qb, q_lag)):
             if i == 5 and stream_i is s_qa:
                 for copy in hid_copies:
                     copy.wait()
@@ -557,10 +548,13 @@
             if 0 <= i - start < STEPS_GATHER:
                 stream_i.step(i - start)
         if i == 0:
+            found_v[...] = find_pages(table_ref[...], length_ref[...])
             for kind in range(2):
                 fresh_kv[kind] = (
                     new_ref[:, :, kind, :].astype(jnp.float32).reshape(steps_reqs, columns)
                 )
+        if i == 4:
+            found_copy.start()
         if i == 5:
             multiply(s_k, wk, acc.at[0], 1)
             multiply(s_k, wk, acc.at[0], -1)
@@ -581,6 +575,7 @@
             vout[...] = clip(acc[1, :, theirs], 1, theirs).reshape(vout.shape)
             values_over.start()
             vbuf[my_pages] = clip(acc[1, :, mine], 1, mine).reshape(vout.shape)
+    found_copy.wait()
     heard(my, 1, column).wait_recv()
     peak = jnp.max(my[...], axis=0)
     smooth_ref[...] = jnp.sqrt(jnp.max(peak, axis=0, keepdims=True) + EPSILON)
@@ -697,7 +692,7 @@
     last.wait()
 
 
-def decode(hidden, key_weight, value_weight, queries, group_scale, new_kv, found):
+def decode(hidden, key_weight, value_weight, queries, group_scale, new_kv, table, lengths):
     tokens, depth = hidden.shape
     rows, columns = key_weight.shape
     step_reqs, q_columns = queries.shape
@@ -706,7 +701,6 @@
     bf16, f32 = jnp.bfloat16, jnp.float32
     any_spec = pl.BlockSpec(memory_space=pl.ANY)
     vmem = pl.BlockSpec(memory_space=pltpu.VMEM)
-    smem = pl.BlockSpec(memory_space=pltpu.SMEM)
     return pl.pallas_call(
         decode_kernel,
         out_shape=(
@@ -714,7 +708,7 @@
             jax.ShapeDtypeStruct((1, columns), f32),
             jax.ShapeDtypeStruct((step_reqs, q_columns), bf16),
         ),
-        in_specs=[any_spec, any_spec, any_spec, any_spec, vmem, vmem, smem],
+        in_specs=[any_spec, any_spec, any_spec, any_spec, vmem, vmem, vmem, vmem],
         out_specs=(vmem, vmem, vmem),
         scratch_shapes=[
             pltpu.VMEM((tokens, depth), bf16),
@@ -729,6 +723,8 @@
             pltpu.VMEM((2 * pages, PAGE, HD), bf16),
             pltpu.VMEM((pages, PAGE, HD), bf16),
             pltpu.VMEM((2, step_reqs, columns), f32),
+            pltpu.VMEM((3 * SLOTS, lengths.shape[1]), jnp.int32),
+            pltpu.SMEM((3 * SLOTS, lengths.shape[1]), jnp.int32),
             pltpu.VMEM((CHIPS + 1, HD, across), f32),
             pltpu.VMEM((CHIPS + 1, 2, across), f32),
             pltpu.VMEM((CHIPS, HD, across), bf16),
@@ -736,7 +732,7 @@
             pltpu.VMEM((2, 2, CHIPS, HD, across), bf16),
             pltpu.VMEM((2, 2, CHIPS, 2, across), f32),
             pltpu.VMEM((step_reqs, q_columns // 2), bf16),
-            pltpu.SemaphoreType.DMA((4,)),
+            pltpu.SemaphoreType.DMA((5,)),
             pltpu.SemaphoreType.DMA((4,)),
             pltpu.SemaphoreType.DMA((4,)),
             pltpu.SemaphoreType.DMA((4, CHIPS)),
@@ -751,7 +747,7 @@
             collective_id=0, has_side_effects=True, vmem_limit_bytes=60 * 2**20
         ),
         name="decode",
-    )(hidden, key_weight, value_weight, queries, group_scale, new_kv, found)
+    )(hidden, key_weight, value_weight, queries, group_scale, new_kv, table, lengths)
 
 
 def finish_kernel(*refs):
@@ -809,7 +805,8 @@
             decode_query.reshape(steps * requests, q_columns),
             group_scale,
             new_kv,
-            find_pages(page_table, lengths),
+            page_table.T,
+            lengths.reshape(1, -1),
         )
     )
     return (

time: 91 us -> 88.6 us (0.974)
  Pallas kernels: 89.7 us -> 87.3 us
    pallas_call x1 -> x0, Pallas kernels: 1.78 us -> none  [find_pages(): pl.pallas_call(find_kernel, out_shape=jax.ShapeDtypeStruct((3 * SLOTS, re...]
where the time goes in v6:
time: 88.6 us; the launch traced here: 88.1 us
  Pallas kernels  87.3 us (99%)
    pallas_call x1, Pallas kernels, decode(): pl.pallas_call(decode_kernel, out_shape=(jax.ShapeDtypeStruct((tokens, 2,...  85.3 us
    pallas_call x1, Pallas kernels, finish(): pl.pallas_call(finish_kernel, out_shape=tuple((jax.ShapeDtypeStruct(a.sha...  2.06 us

profile of v6, /device:TPU:1, one launch (start us, length us, event | category | flops | bytes accessed | tf_op | source)
XLA Modules:
  0.0 88.1 jit_solution(17844910456856942697)
XLA Ops:
  0.6 85.3 %decode.1 = (bf16[1024,2,256]{2,1,0:T(2,128)(2,1)}, f32[1,256]{1,0:T(1,128)}, bf16[32,2048]{1,0:T(8,128)(2,1)}) custom-call(bf16[1024,8192]{1,0:T(8,128)(2,1)} %hidden_hbm.1, bf16[128,256]{1,0:T(8,128)(2,1)} %wk_hbm.1, bf16[128,256]{1,0:T(8,128)(2,1)} %wv_hbm.1, bf16[32,2048]{1,0:T(8,128)(2,1)} %bitcast.5, f32[2,256]{1,0:T(2,128)} %scale_ref.1, ...), custom_call_target="tpu_custom_call" | custom-call | tf_op jit(solution)/shard_map/decode/pallas_call | solution.py:704
  85.9 2.1 %finish.1 = (bf16[1024,2,256]{2,1,0:T(2,128)(2,1)}, f32[1,256]{1,0:T(1,128)}, bf16[32,2048]{1,0:T(8,128)(2,1)}) custom-call(bf16[1024,2,256]{2,1,0:T(2,128)(2,1)} %get-tuple-element.9.refs_0_, f32[1,256]{1,0:T(1,128)} %get-tuple-element.10.refs_1_, bf16[32,2048]{1,0:T(8,128)(2,1)} %get-tuple-element.11.refs_2_), custom_call_target="tpu_custom_call" | custom-call | tf_op jit(solution)/shard_map/finish/pallas_call | solution.py:782

commit v7 on v6

--- a/solution.py
+++ b/solution.py
@@ -560,7 +560,7 @@
             multiply(s_k, wk, acc.at[0], -1)
         if i == 6:
             multiply(s_k, wk, acc.at[0], 2)
-            mz[place] = jnp.max(jnp.abs(acc[0]).reshape(tokens // 8, 8, columns), axis=0)
+            mz[place] = jnp.max(jnp.abs(acc[0]), axis=0, keepdims=True)
             tell(mz, place, 0, ring)
             keys_over.start()
             multiply(s_v, wv, acc.at[1], 0)
@@ -578,7 +578,7 @@
     found_copy.wait()
     heard(my, 1, column).wait_recv()
     peak = jnp.max(my[...], axis=0)
-    smooth_ref[...] = jnp.sqrt(jnp.max(peak, axis=0, keepdims=True) + EPSILON)
+    smooth_ref[...] = jnp.sqrt(peak + EPSILON)
     my_smooth = smooth_ref[:, mine]
 
     def queries_of(g):
@@ -714,8 +714,8 @@
             pltpu.VMEM((tokens, depth), bf16),
             pltpu.VMEM((CHIPS, 2, rows, columns), bf16),
             pltpu.VMEM((CHIPS, 2, rows, columns), bf16),
-            pltpu.VMEM((2 * NZ, 8, columns), f32),
-            pltpu.VMEM((NY, 8, columns), f32),
+            pltpu.VMEM((2 * NZ, 1, columns), f32),
+            pltpu.VMEM((NY, 1, columns), f32),
             pltpu.VMEM((CHIPS, 2, step_reqs // 2, q_columns // 2), bf16),
             pltpu.VMEM((2, tokens, columns), f32),
             pltpu.VMEM((tokens, HD), f32),

time: 88.6 us -> 88.8 us (level)
  no operation moved by 1% of the time
where the time goes in v7:
time: 88.8 us; the launch traced here: 87.7 us
  Pallas kernels  86.9 us (98%)
    pallas_call x1, Pallas kernels, decode(): pl.pallas_call(decode_kernel, out_shape=(jax.ShapeDtypeStruct((tokens, 2,...  84.8 us
    pallas_call x1, Pallas kernels, finish(): pl.pallas_call(finish_kernel, out_shape=tuple((jax.ShapeDtypeStruct(a.sha...  2.06 us

profile of v7, /device:TPU:1, one launch (start us, length us, event | category | flops | bytes accessed | tf_op | source)
XLA Modules:
  0.0 87.7 jit_solution(1663134097913459285)
XLA Ops:
  0.6 84.8 %decode.1 = (bf16[1024,2,256]{2,1,0:T(2,128)(2,1)}, f32[1,256]{1,0:T(1,128)}, bf16[32,2048]{1,0:T(8,128)(2,1)}) custom-call(bf16[1024,8192]{1,0:T(8,128)(2,1)} %hidden_hbm.1, bf16[128,256]{1,0:T(8,128)(2,1)} %wk_hbm.1, bf16[128,256]{1,0:T(8,128)(2,1)} %wv_hbm.1, bf16[32,2048]{1,0:T(8,128)(2,1)} %bitcast.5, f32[2,256]{1,0:T(2,128)} %scale_ref.1, ...), custom_call_target="tpu_custom_call" | custom-call | tf_op jit(solution)/shard_map/decode/pallas_call | solution.py:704
  85.4 2.1 %finish.1 = (bf16[1024,2,256]{2,1,0:T(2,128)(2,1)}, f32[1,256]{1,0:T(1,128)}, bf16[32,2048]{1,0:T(8,128)(2,1)}) custom-call(bf16[1024,2,256]{2,1,0:T(2,128)(2,1)} %get-tuple-element.9.refs_0_, f32[1,256]{1,0:T(1,128)} %get-tuple-element.10.refs_1_, bf16[32,2048]{1,0:T(8,128)(2,1)} %get-tuple-element.11.refs_2_), custom_call_target="tpu_custom_call" | custom-call | tf_op jit(solution)/shard_map/finish/pallas_call | solution.py:782
